TPU v7x, 32 devices: a whole 2x2x4 slice. The times are simulated.
32 devices in a mesh: gy: 8 (over z, core), gz: 4 (over y, x).
Axes of the slice: x: 2, y: 2, z: 4, core: 2. Of those that a mesh axis runs over, the one named last changes fastest.
Arguments:
- measured: float32 [4, 1024, 1024], P('gz', 'gy'), may hold values from -20 to 20
- point_spread: float32 [1024, 1024], P('gy'), may hold values from -0.005859375 to 0.005859375
- stencil_weights: float32 [3, 3, 3], replicated, may hold values from -0.9 to 0.9
- upstream: float32 [4, 1024, 1024], P('gz', 'gy'), may hold values from -6 to 6
Outputs:
- grad_measured: float32 [4, 1024, 1024], P('gz', 'gy')
- grad_stencil: float32 [3, 3, 3], replicated
All inputs are finite; a program needn't handle non-finite values.
Results may differ from a plain program's by a relative error of at most 0.00021.
Values sent between devices are 32-bit elements; how exact they have to be, the bound alone decides.
A program may use at most 64 MiB of HBM per device.

v0:
```python
import math

import jax
import jax.numpy as jnp
from jax import lax
from jax.experimental import pallas as pl
from jax.experimental.pallas import tpu as pltpu
from jax.sharding import PartitionSpec as P

MESH = pl.DeviceIdType.MESH
SIDES = [(dy, dz) for dy in (-1, 0, 1) for dz in (-1, 0, 1) if (dy, dz) != (0, 0)]
VMEM = pl.BlockSpec(memory_space=pltpu.VMEM)
SMEM = pl.BlockSpec(memory_space=pltpu.SMEM)


def moved(value, shift):
    if shift == 0:
        return value
    width = value.shape[1]
    lane = lax.broadcasted_iota(jnp.int32, value.shape, 1)
    edge = 0 if shift > 0 else width - 1
    return jnp.where(lane == edge, 0.0, pltpu.roll(value, shift % width, 1))


def regular_kernel(count_y, count_z, weights, volume, back, grown, mapped, shifted, send, receive):
    rows, columns = volume.shape
    y, z = (lax.axis_index("gy"), lax.axis_index("gz"))

    def there(dy, dz):
        return (y + dy >= 0) & (y + dy < count_y) & (z + dz >= 0) & (z + dz < count_z)

    barrier = pltpu.get_barrier_semaphore()
    for dy, dz in SIDES:

        @pl.when(there(dy, dz))
        def _():
            pl.semaphore_signal(barrier, inc=1, device_id=(y + dy, z + dz), device_id_type=MESH)

    def span(place, count):
        return 1 + jnp.where(place > 0, 1, 0) + jnp.where(place < count - 1, 1, 0)

    pl.semaphore_wait(barrier, span(y, count_y) * span(z, count_z) - 1)

    def copy(field, phase, number):
        dy, dz = SIDES[number]
        source = field.at[1, pl.ds(rows if dy > 0 else 8, 8 if dy else rows)]
        start = 8 if dy == 0 else 0 if dy > 0 else rows + 8
        return pltpu.make_async_remote_copy(
            src_ref=source,
            dst_ref=field.at[1 - dz, pl.ds(start, 8 if dy else rows)],
            send_sem=send.at[phase, number],
            recv_sem=receive.at[phase, number],
            device_id=(y + dy, z + dz),
            device_id_type=MESH,
        )

    def exchange(field, phase):
        for number, (dy, dz) in enumerate(SIDES):

            @pl.when(there(dy, dz))
            def _():
                copy(field, phase, number).start()

        for number, (dy, dz) in enumerate(SIDES):
            start = 8 if dy == 0 else 0 if dy > 0 else rows + 8

            @pl.when(jnp.logical_not(there(-dy, -dz)))
            def _():
                field[1 - dz, pl.ds(start, 8 if dy else rows)] = jnp.zeros(
                    (8 if dy else rows, columns), jnp.float32
                )

        for number, (dy, dz) in enumerate(SIDES):

            @pl.when(there(-dy, -dz))
            def _():
                copy(field, phase, number).wait_recv()

            @pl.when(there(dy, dz))
            def _():
                copy(field, phase, number).wait_send()

    def apply(field, flip, put):
        def weight(a, b, c):
            return weights[26 - (9 * a + 3 * b + c) if flip else 9 * a + 3 * b + c]

        @pl.loop(0, (rows + 16) // 8)
        def _(step):
            here = pl.ds(pl.multiple_of(step * 8, 8), 8)
            sums = [None] * 3
            for a in range(3):
                value = field[a, here]
                for c in range(3):
                    turned = moved(value, 1 - c)
                    for b in range(3):
                        term = weight(a, b, c) * turned
                        sums[b] = term if sums[b] is None else sums[b] + term
            for b in range(3):
                shifted[b, here] = sums[b]

        @pl.loop(0, rows // 8)
        def _(step):
            first = pl.multiple_of(step * 8, 8)
            around = pl.ds(first, 24)
            total = shifted[1, pl.ds(first + 8, 8)]
            total = total + shifted[0, around][7:15] + shifted[2, around][9:17]
            put(first, total)

    @pl.loop(0, rows // 8)
    def _(step):
        first = pl.multiple_of(step * 8, 8)
        grown[1, pl.ds(first + 8, 8)] = volume[pl.ds(first, 8)]

    exchange(grown, 0)

    def put_mapped(first, total):
        mapped[1, pl.ds(first + 8, 8)] = total

    apply(grown, False, put_mapped)
    exchange(mapped, 1)

    def put_back(first, total):
        back[pl.ds(first, 8)] = total

    apply(mapped, True, put_back)


def regular(volume, kernel):
    rows, columns = volume.shape[1:]
    count_y, count_z = (lax.axis_size("gy"), lax.axis_size("gz"))
    field = jax.ShapeDtypeStruct((3, rows + 16, columns), jnp.float32)

    def body(*refs):
        regular_kernel(count_y, count_z, *refs)

    back, grown, mapped = pl.pallas_call(
        body,
        out_shape=(jax.ShapeDtypeStruct((rows, columns), jnp.float32), field, field),
        in_specs=[SMEM, VMEM],
        out_specs=(VMEM, VMEM, VMEM),
        scratch_shapes=[
            pltpu.VMEM((3, rows + 16, columns), jnp.float32),
            pltpu.SemaphoreType.DMA((2, 8)),
            pltpu.SemaphoreType.DMA((2, 8)),
        ],
        cost_estimate=pl.CostEstimate(flops=120 * rows * columns, bytes_accessed=20 * rows * columns, transcendentals=0),
        compiler_params=pltpu.CompilerParams(collective_id=0, has_side_effects=True),
        name="regular",
    )(kernel.reshape(27), volume[0])
    return (back[None], grown, mapped)


def total_kernel(count_y, count_z, value, out, column, row, across, send, receive):
    y, z = (lax.axis_index("gy"), lax.axis_index("gz"))
    along_y = [(lax.rem(y + k, count_y), z) for k in range(1, count_y)]
    along_z = [(y, lax.rem(z + k, count_z)) for k in range(1, count_z)]
    barrier = pltpu.get_barrier_semaphore()
    for place in along_y + along_z:
        pl.semaphore_signal(barrier, inc=1, device_id=place, device_id_type=MESH)
    pl.semaphore_wait(barrier, count_y + count_z - 2)

    def gather(source, slots, places, base):
        copies = []
        for k, place in enumerate(places):
            copies.append(
                pltpu.make_async_remote_copy(
                    src_ref=source,
                    dst_ref=slots.at[k],
                    send_sem=send.at[base + k],
                    recv_sem=receive.at[base + k],
                    device_id=place,
                    device_id_type=MESH,
                )
            )
            copies[-1].start()
        for item in copies:
            item.wait()

    def ordered(own, slots, index, count):
        total = jnp.zeros_like(own)
        for j in range(count):
            term = own
            for k in range(1, count):
                term = jnp.where(lax.rem(index - j + count, count) == k, slots[k - 1], term)
            total = total + term
        return total

    gather(value, column, along_y, 0)
    across[...] = ordered(value[...], column, y, count_y)
    gather(across, row, along_z, count_y - 1)
    out[...] = ordered(across[...], row, z, count_z)


def total(values, collective):
    count_y, count_z = (lax.axis_size("gy"), lax.axis_size("gz"))
    count = values.shape[0]

    def body(*refs):
        total_kernel(count_y, count_z, *refs)

    block = jnp.broadcast_to(jnp.pad(values, (0, 128 - count))[None], (8, 128))
    copies = count_y + count_z - 2
    summed = pl.pallas_call(
        body,
        out_shape=jax.ShapeDtypeStruct((8, 128), jnp.float32),
        in_specs=[VMEM],
        out_specs=VMEM,
        scratch_shapes=[
            pltpu.VMEM((count_y - 1, 8, 128), jnp.float32),
            pltpu.VMEM((count_z - 1, 8, 128), jnp.float32),
            pltpu.VMEM((8, 128), jnp.float32),
            pltpu.SemaphoreType.DMA((copies,)),
            pltpu.SemaphoreType.DMA((copies,)),
        ],
        compiler_params=pltpu.CompilerParams(collective_id=collective, has_side_effects=True),
        name="total",
    )(block)
    return summed[0, :count]


def correlate_kernel(scalars, grown_0, grown_1, grown_2, grown_up, mapped_0, mapped_1, mapped_2, mapped_up, out):
    rows = grown_0.shape[1] - 16
    columns = grown_0.shape[2]
    c_up, c_zero, c_one, c_two, d_zero, d_one, s_zero, s_grad, s_direction = (scalars[k] for k in range(9))
    out[...] = jnp.zeros_like(out)

    @pl.loop(0, rows // 8)
    def _(step):
        first = pl.multiple_of(step * 8, 8)
        here = pl.ds(first + 8, 8)
        zero, one = (mapped_0[1, here], mapped_1[1, here])
        grad = c_up * mapped_up[1, here] + c_zero * zero + c_one * one + c_two * mapped_2[1, here]
        values = (
            s_zero * zero + s_grad * grad,
            s_grad * zero,
            s_direction * (d_zero * zero + d_one * one),
        )
        turned = [[moved(value, c - 1) for value in values] for c in range(3)]
        for a in range(3):
            around = pl.ds(first, 24)
            full_0, full_1 = (grown_0[a, around], grown_1[a, around])
            full_grad = c_up * grown_up[a, around] + c_zero * full_0 + c_one * full_1 + c_two * grown_2[a, around]
            full_direction = d_zero * full_0 + d_one * full_1
            for b in range(3):
                fields = [item[7 + b : 15 + b] for item in (full_0, full_grad, full_direction)]
                for c in range(3):
                    product = turned[c][0] * fields[0] + turned[c][1] * fields[1] + turned[c][2] * fields[2]
                    folded = product[:, :128]
                    for part in range(1, columns // 128):
                        folded = folded + product[:, 128 * part : 128 * part + 128]
                    out[9 * a + 3 * b + c] += folded


def correlate(scalars, *fields):
    return pl.pallas_call(
        correlate_kernel,
        out_shape=jax.ShapeDtypeStruct((27, 8, 128), jnp.float32),
        in_specs=[SMEM] + [VMEM] * 8,
        out_specs=VMEM,
        cost_estimate=pl.CostEstimate(flops=40000000, bytes_accessed=8000000, transcendentals=0),
        name="correlate",
    )(scalars, *fields).sum((1, 2))


def contract(form, left, right):
    return jnp.einsum(form, left, right, precision=lax.Precision.HIGH)


def wave_tables(length, groups):
    half = length // 2
    bins = half // groups
    pair = groups // 2
    shape = (half, pair, 2, bins)
    place = lax.broadcasted_iota(jnp.int32, shape, 0)
    part = lax.broadcasted_iota(jnp.int32, shape, 2)
    slot = lax.broadcasted_iota(jnp.int32, shape, 1) * bins + lax.broadcasted_iota(jnp.int32, shape, 3)
    tables = []
    for odd in range(2):
        frequency = 2 * slot + odd
        steps = place * frequency + part * (length // 4)
        if not odd:
            steps = jnp.where((slot == 0) & (part == 1), place * half, steps)
        angle = (steps % length).astype(jnp.float32) * (2.0 * math.pi / length)
        tables.append(jnp.cos(angle).reshape(half, pair, 2 * bins))
    return tables


def combine(raw, on_row, on_lane):
    even, odd = raw
    a, b, c, d = (
        jnp.concatenate([piece[:, part, :, :, side] for piece in (even, odd)], 0)
        for part, side in ((0, 0), (0, 1), (1, 0), (1, 1))
    )
    special = on_row | on_lane
    plus_real = jnp.where(special, a, a - d)
    plus_imaginary = jnp.where(on_row, b, jnp.where(on_lane, c, b + c))
    minus_real = jnp.where(on_row, c, jnp.where(on_lane, b, a + d))
    minus_imaginary = jnp.where(special, d, b - c)
    return (jnp.stack([plus_real, minus_real]), jnp.stack([plus_imaginary, minus_imaginary]))


def separate(spectrum, on_row, on_lane):
    (plus_real, minus_real), (plus_imaginary, minus_imaginary) = spectrum
    special = on_row | on_lane
    a = jnp.where(special, plus_real, plus_real + minus_real)
    d = jnp.where(special, minus_imaginary, minus_real - plus_real)
    b = jnp.where(on_row, plus_imaginary, jnp.where(on_lane, minus_real, plus_imaginary + minus_imaginary))
    c = jnp.where(on_row, minus_real, jnp.where(on_lane, plus_imaginary, plus_imaginary - minus_imaginary))
    scale = jnp.where(on_row & on_lane, 1.0, 2.0)
    a, b, c, d = (value * scale for value in (a, b, c, d))
    whole = jnp.stack([jnp.stack([a, b], 3), jnp.stack([c, d], 3)], 1)
    pair = whole.shape[0] // 2
    return (whole[:pair], whole[pair:])


def times(left, right, corner, conjugate=False):
    (a, b), (c, d) = (left, right)
    cross = b * d
    sign = -1.0 if conjugate else 1.0
    real = jnp.where(corner, a * c, a * c - sign * cross)
    imaginary = jnp.where(corner, cross, sign * a * d + b * c)
    return (real, imaginary)


def linear(*terms):
    total_real = total_imaginary = 0.0
    for scale, (real, imaginary) in terms:
        scale_real, scale_imaginary = scale if isinstance(scale, tuple) else (scale, scale)
        total_real = total_real + scale_real * real
        total_imaginary = total_imaginary + scale_imaginary * imaginary
    return (total_real, total_imaginary)


def local(measured, point_spread, stencil_weights, upstream):
    planes, row_count, columns = measured.shape
    groups = lax.axis_size("gy")
    rows = row_count * groups
    cells = planes * rows * columns * lax.axis_size("gz")
    bins = columns // 2 // groups
    even_x, odd_x = wave_tables(columns, groups)
    even_y, odd_y = (even_x, odd_x) if rows == columns else wave_tables(rows, groups)
    y_bins = rows // 2 // groups
    spectral = (groups, y_bins, 1, bins)
    on_row = (lax.broadcasted_iota(jnp.int32, spectral, 0) == 0) & (
        lax.broadcasted_iota(jnp.int32, spectral, 1) == 0
    )
    on_lane = (lax.broadcasted_iota(jnp.int32, spectral, 3) == 0) & (lax.axis_index("gy") == 0)
    corner = on_row & on_lane

    def forward(volumes):
        count = volumes.shape[0]
        low, high = (volumes[:, :, : columns // 2], volumes[:, :, columns // 2 :])
        sent = jnp.concatenate(
            [contract("vrj,jdl->drvl", low + high, even_x), contract("vrj,jdl->drvl", low - high, odd_x)], 0
        )
        arrived = lax.all_to_all(
            sent.reshape(groups, row_count, count * 2 * bins), "gy", split_axis=0, concat_axis=0, tiled=True
        )
        arrived = arrived.reshape(rows, count * 2 * bins)
        low, high = (arrived[: rows // 2], arrived[rows // 2 :])
        raw = [
            contract("jds,jl->dsl", table, value).reshape(groups // 2, 2, y_bins, count, 2, bins)
            for table, value in ((even_y, low + high), (odd_y, low - high))
        ]
        return combine(raw, on_row, on_lane)

    def inverse(spectrum):
        count = spectrum[0].shape[3]
        pieces = separate(spectrum, on_row, on_lane)
        one, two = (
            contract("jds,dsl->jl", table, piece.reshape(groups // 2, 2 * y_bins, count * 2 * bins))
            for table, piece in ((even_y, pieces[0]), (odd_y, pieces[1]))
        )
        sent = jnp.concatenate([one + two, one - two], 0).reshape(groups, row_count, count * 2 * bins)
        arrived = lax.all_to_all(sent, "gy", split_axis=0, concat_axis=0, tiled=True)
        arrived = arrived.reshape(groups, row_count, count, 2 * bins)
        one = contract("drvl,jdl->vrj", arrived[: groups // 2], even_x)
        two = contract("drvl,jdl->vrj", arrived[groups // 2 :], odd_x)
        return jnp.concatenate([one + two, one - two], 2) / float(rows * columns)

    def pick(spectrum, start, count):
        return tuple(lax.slice_in_dim(part, start, start + count, axis=3) for part in spectrum)

    def join(*spectra):
        return tuple(jnp.concatenate(parts, 3) for parts in zip(*spectra))

    spectra = forward(jnp.concatenate([point_spread[None], measured], 0))
    transfer = pick(spectra, 0, 1)
    squares = (transfer[0] ** 2, transfer[1] ** 2)
    gain = (
        jnp.where(corner, squares[0], squares[0] + squares[1]),
        jnp.where(corner, squares[1], squares[0] + squares[1]),
    )
    spectrum_0 = times(pick(spectra, 1, planes), transfer, corner, True)
    blurred_0 = linear((gain, spectrum_0))
    pair = inverse(join(spectrum_0, blurred_0))
    vector_0 = pair[:planes]
    back_0, grown_0, mapped_0 = regular(vector_0, stencil_weights)
    back_up, grown_up, mapped_up = regular(upstream, stencil_weights)
    vector_1 = pair[planes:] + back_0
    spectrum_1 = linear((1.0, blurred_0), (1.0, forward(back_0)))
    blurred_1 = linear((gain, spectrum_1))
    early = forward(jnp.concatenate([upstream, back_up], 0))
    back_1, grown_1, mapped_1 = regular(vector_1, stencil_weights)
    vector_2 = inverse(blurred_1) + back_1
    norm_0, curve_0, image_0, up_0, up_1 = total(
        jnp.stack(
            [
                jnp.sum(vector_0 * vector_0),
                jnp.sum(vector_0 * vector_1),
                jnp.sum(vector_1 * vector_1),
                jnp.sum(upstream * vector_0),
                jnp.sum(upstream * vector_1),
            ]
        ),
        1,
    )
    step_0 = norm_0 / curve_0
    residual = vector_0 - step_0 * vector_1
    residual_image = vector_1 - step_0 * vector_2
    norm_1, cross, inner, up_residual, image_cross = total(
        jnp.stack(
            [
                jnp.sum(residual * residual),
                jnp.sum(residual * vector_1),
                jnp.sum(residual * residual_image),
                jnp.sum(upstream * residual),
                jnp.sum(residual_image * vector_1),
            ]
        ),
        2,
    )
    back_2, grown_2, mapped_2 = regular(vector_2, stencil_weights)
    late = forward(jnp.concatenate([back_1, back_2], 0))
    ratio = norm_1 / norm_0
    curve_1 = inner + 2.0 * ratio * cross + ratio * ratio * curve_0
    step_1 = norm_1 / curve_1
    grad_step_1 = up_residual + ratio * up_0
    grad_curve_1 = -grad_step_1 * step_1 / curve_1
    grad_ratio = step_1 * up_0 + 2.0 * grad_curve_1 * (cross + ratio * curve_0)
    known_image = step_1 * up_1 + 2.0 * grad_curve_1 * (image_cross + ratio * image_0)
    grad_norm = grad_step_1 / curve_1 + grad_ratio / norm_0
    grad_step_0 = up_0 - known_image - 2.0 * grad_norm * cross
    grad_curve_0 = -grad_step_0 * step_0 / curve_0
    grad_norm_0 = -grad_ratio * ratio / norm_0 + grad_step_0 / curve_0

    spectrum_2 = linear((1.0, linear((gain, spectrum_1))), (1.0, pick(late, 0, planes)))
    spectrum_up = pick(early, 0, planes)
    residual_terms = ((1.0, spectrum_0), (-step_0, spectrum_1))
    direction_image = linear((1.0 + ratio, spectrum_1), (-step_0, spectrum_2))
    grad_direction = linear((step_1, spectrum_up), (2.0 * grad_curve_1, direction_image))
    grad_residual = linear((1.0, grad_direction), (2.0 * grad_norm, linear(*residual_terms)))
    grad_back = linear(
        (step_1, pick(early, planes, planes)),
        (2.0 * grad_curve_1 * (1.0 + ratio) - 2.0 * grad_norm * step_0, pick(late, 0, planes)),
        (-2.0 * grad_curve_1 * step_0, pick(late, planes, planes)),
        (2.0 * grad_norm, linear((1.0, spectrum_1), (-1.0, blurred_0))),
    )
    grad_right = linear(
        (step_0, spectrum_up),
        (ratio, grad_direction),
        (2.0 * grad_curve_0, spectrum_1),
        (2.0 * grad_norm_0, spectrum_0),
        (1.0, grad_residual),
        (-step_0, linear((gain, grad_residual), (1.0, grad_back))),
    )
    grad_measured = inverse(times(grad_right, transfer, corner))

    terms = correlate(
        jnp.stack(
            [
                step_1,
                2.0 * grad_norm,
                2.0 * grad_curve_1 * (1.0 + ratio) - 2.0 * grad_norm * step_0,
                -2.0 * grad_curve_1 * step_0,
                1.0 + ratio,
                -step_0,
                2.0 * grad_curve_0,
                -step_0,
                2.0 * grad_curve_1,
            ]
        ),
        grown_0, grown_1, grown_2, grown_up, mapped_0, mapped_1, mapped_2, mapped_up,
    )
    grad_stencil = total(terms, 3).reshape(3, 3, 3) / math.sqrt(cells)
    return (grad_measured, grad_stencil)


def solution(mesh):
    return jax.shard_map(
        local,
        mesh=mesh,
        in_specs=(P("gz", "gy", None), P("gy", None), P(), P("gz", "gy", None)),
        out_specs=(P("gz", "gy", None), P()),
        check_vma=False,
    )
```

profile of v0, /device:TPU:0, one launch (start us, length us, event | category | flops | bytes accessed | tf_op | source)
XLA Modules:
  0.0 642.9 jit_solution(5269032823555812526)
XLA Ops:
  1.1 6.0 convolution_bitcast_fusion.10
  13.5 6.5 %all-to-all-start = ((f32[8,128,256]{2,1,0:T(8,128)}), f32[8,128,256]{2,1,0:T(8,128)S(1)}, u32[]{:S(2)}, u32[]{:S(2)}) async-start(f32[8,128,256]{2,1,0:T(8,128)} %copy.150), calls=%async_computation | async-start | bytes 2097152 | tf_op jit(solution)/shard_map/all_to_all | solution.py:356
  24.3 22.1 %all-to-all-done = f32[8,128,256]{2,1,0:T(8,128)S(1)} async-done(((f32[8,128,256]{2,1,0:T(8,128)}), f32[8,128,256]{2,1,0:T(8,128)S(1)}, u32[]{:S(2)}, u32[]{:S(2)}) %all-to-all-start) | async-done | bytes 1048608 | tf_op jit(solution)/shard_map/all_to_all | solution.py:356
  52.0 5.8 fusion.30
  66.3 6.4 convolution_bitcast_fusion.8
  75.1 5.9 fusion.269
  86.6 25.9 %all-to-all-done.1 = f32[8,128,256]{1,2,0:T(8,128)S(1)} async-done(((f32[8,128,256]{1,2,0:T(8,128)}), f32[8,128,256]{1,2,0:T(8,128)S(1)}, u32[]{:S(2)}, u32[]{:S(2)}) %all-to-all-start.1) | async-done | bytes 1048608 | tf_op jit(solution)/shard_map/all_to_all | solution.py:375
  123.8 49.7 %regular.4 = (f32[128,1024]{1,0:T(8,128)}, f32[3,144,1024]{2,1,0:T(8,128)}, f32[3,144,1024]{2,1,0:T(8,128)}) custom-call(f32[27]{0:T(128)} %reshape.2572.refs_0_, f32[128,1024]{1,0:T(8,128)} %slice_bitcast_fusion.refs_1_), custom_call_target="tpu_custom_call" | custom-call | flops 15728640 | bytes 2621440 | tf_op jit(solution)/shard_map/regular/pallas_call | solution.py:136
  173.5 5.9 convolution_bitcast_fusion.21
  185.1 14.1 %all-to-all-start.3 = ((f32[8,128,128]{1,2,0:T(8,128)}), f32[8,128,128]{1,2,0:T(8,128)}, u32[]{:S(2)}, u32[]{:S(2)}) async-start(f32[8,128,128]{1,2,0:T(8,128)} %maximum_bitcast_fusion.2), calls=%async_computation.3 | async-start | bytes 1048576 | tf_op jit(solution)/shard_map/all_to_all | solution.py:356
  204.7 9.9 %all-to-all-done.3 = f32[8,128,128]{1,2,0:T(8,128)} async-done(((f32[8,128,128]{1,2,0:T(8,128)}), f32[8,128,128]{1,2,0:T(8,128)}, u32[]{:S(2)}, u32[]{:S(2)}) %all-to-all-start.3) | async-done | bytes 524320 | tf_op jit(solution)/shard_map/all_to_all | solution.py:356
  232.2 6.1 convolution_bitcast_fusion.18
  241.6 5.7 fusion.273
  252.3 52.1 %regular.5 = (f32[128,1024]{1,0:T(8,128)}, f32[3,144,1024]{2,1,0:T(8,128)}, f32[3,144,1024]{2,1,0:T(8,128)}) custom-call(f32[27]{0:T(128)} %reshape.2572.refs_0_, f32[128,1024]{1,0:T(8,128)} %bitcast.518), custom_call_target="tpu_custom_call" | custom-call | flops 15728640 | bytes 2621440 | tf_op jit(solution)/shard_map/regular/pallas_call | solution.py:136
  304.4 6.0 convolution_bitcast_fusion.6
  319.0 17.3 %all-to-all-start.2 = ((f32[8,128,256]{2,1,0:T(8,128)}), f32[8,128,256]{2,1,0:T(8,128)}, u32[]{:S(2)}, u32[]{:S(2)}) async-start(f32[8,128,256]{2,1,0:T(8,128)} %copy.183), calls=%async_computation.2 | async-start | bytes 2097152 | tf_op jit(solution)/shard_map/all_to_all | solution.py:356
  344.4 24.5 %total.3 = f32[8,128]{1,0:T(8,128)} custom-call(f32[8,128]{1,0:T(8,128)} %broadcast_in_dim.168.refs_0_), custom_call_target="tpu_custom_call" | custom-call | tf_op jit(solution)/shard_map/total/pallas_call | solution.py:203
  371.8 48.6 %regular.6 = (f32[128,1024]{1,0:T(8,128)}, f32[3,144,1024]{2,1,0:T(8,128)}, f32[3,144,1024]{2,1,0:T(8,128)}) custom-call(f32[27]{0:T(128)} %reshape.2572.refs_0_, f32[128,1024]{1,0:T(8,128)} %bitcast.519), custom_call_target="tpu_custom_call" | custom-call | flops 15728640 | bytes 2621440 | tf_op jit(solution)/shard_map/regular/pallas_call | solution.py:136
  433.4 62.1 %regular.7 = (f32[128,1024]{1,0:T(8,128)}, f32[3,144,1024]{2,1,0:T(8,128)}, f32[3,144,1024]{2,1,0:T(8,128)}) custom-call(f32[27]{0:T(128)} %reshape.2572.refs_0_, f32[128,1024]{1,0:T(8,128)} %get-tuple-element.45.refs_1_), custom_call_target="tpu_custom_call" | custom-call | flops 15728640 | bytes 2621440 | tf_op jit(solution)/shard_map/regular/pallas_call | solution.py:136
  495.6 6.0 convolution_bitcast_fusion.2
  510.1 17.3 %all-to-all-start.5 = ((f32[8,128,256]{2,1,0:T(8,128)}), f32[8,128,256]{2,1,0:T(8,128)}, u32[]{:S(2)}, u32[]{:S(2)}) async-start(f32[8,128,256]{2,1,0:T(8,128)} %copy.210), calls=%async_computation.5 | async-start | bytes 2097152 | tf_op jit(solution)/shard_map/all_to_all | solution.py:356
  544.4 15.6 %total.4 = f32[8,128]{1,0:T(8,128)} custom-call(f32[8,128]{1,0:T(8,128)} %broadcast_in_dim.172.refs_0_), custom_call_target="tpu_custom_call" | custom-call | tf_op jit(solution)/shard_map/total/pallas_call | solution.py:203
  606.1 11.9 %correlate.1 = f32[27,8,128]{2,1,0:T(8,128)} custom-call(f32[9]{0:T(128)} %stack.204.scalars, f32[3,144,1024]{2,1,0:T(8,128)} %get-tuple-element.18.grown_0, f32[3,144,1024]{2,1,0:T(8,128)} %get-tuple-element.19.grown_1, f32[3,144,1024]{2,1,0:T(8,128)} %get-tuple-element.20.grown_2, f32[3,144,1024]{2,1,0:T(8,128)} %get-tuple-element.21.grown_up, ...), custom_call_target="tpu_custom_call" | custom-call | flops 40000000 | bytes 8000000 | tf_op jit(solution)/shard_map/correlate/pallas_call | solution.py:255
  619.8 11.4 %total.5 = f32[8,128]{1,0:T(8,128)} custom-call(f32[8,128]{1,0:T(8,128)} %broadcast_in_dim.175.refs_0_), custom_call_target="tpu_custom_call" | custom-call | tf_op jit(solution)/shard_map/total/pallas_call | solution.py:203
  (312 shorter events, 183.1 us)
Async XLA Ops:
  0.6 198.6 %copy-start.62 = (s32[4]{0:T(128)}, s32[4]{0:T(128)S(1)}, u32[]{:S(2)}) copy-start(s32[4]{0:T(128)S(1)} %iota_multiply_fusion.3) | copy-start | bytes 52
  0.7 198.6 %copy-start.57 = (s32[512]{0:T(512)}, s32[512]{0:T(512)S(1)}, u32[]{:S(2)}) copy-start(s32[512]{0:T(512)S(1)} %get-tuple-element.165) | copy-start | bytes 6148
  0.8 178.6 %copy-start.67 = (s32[128]{0:T(128)}, s32[128]{0:T(128)S(1)}, u32[]{:S(2)}) copy-start(s32[128]{0:T(128)S(1)} %iota.818) | copy-start | bytes 1540
  0.9 178.5 %copy-start.72 = (s32[128]{0:T(128)}, s32[128]{0:T(128)S(1)}, u32[]{:S(2)}) copy-start(s32[128]{0:T(128)S(1)} %iota.809) | copy-start | bytes 1540
  1.1 172.4 %copy-start.81 = (pred[128]{0:T(512)(128)(4,1)}, pred[128]{0:T(512)(128)(4,1)S(1)}, u32[]{:S(2)}) copy-start(pred[128]{0:T(512)(128)(4,1)S(1)} %iota.813) | copy-start | bytes 388
  13.5 32.9 %all-to-all-start = ((f32[8,128,256]{2,1,0:T(8,128)}), f32[8,128,256]{2,1,0:T(8,128)S(1)}, u32[]{:S(2)}, u32[]{:S(2)}) async-start(f32[8,128,256]{2,1,0:T(8,128)} %copy.150), calls=%async_computation | async-start | bytes 2097152 | tf_op jit(solution)/shard_map/all_to_all | solution.py:356
  20.2 40.0 %copy-start.47 = (pred[8,64,64]{2,1,0:T(8,128)(4,1)}, pred[8,64,64]{2,1,0:T(8,128)(4,1)S(1)}, u32[]{:S(2)}) copy-start(pred[8,64,64]{2,1,0:T(8,128)(4,1)S(1)} %get-tuple-element.156) | copy-start | bytes 98308
  66.3 6.4 copy-start.17
  82.4 30.1 %all-to-all-start.1 = ((f32[8,128,256]{1,2,0:T(8,128)}), f32[8,128,256]{1,2,0:T(8,128)S(1)}, u32[]{:S(2)}, u32[]{:S(2)}) async-start(f32[8,128,256]{1,2,0:T(8,128)} %copy.174), calls=%async_computation.1 | async-start | bytes 2097152 | tf_op jit(solution)/shard_map/all_to_all | solution.py:375
  185.1 29.6 %all-to-all-start.3 = ((f32[8,128,128]{1,2,0:T(8,128)}), f32[8,128,128]{1,2,0:T(8,128)}, u32[]{:S(2)}, u32[]{:S(2)}) async-start(f32[8,128,128]{1,2,0:T(8,128)} %maximum_bitcast_fusion.2), calls=%async_computation.3 | async-start | bytes 1048576 | tf_op jit(solution)/shard_map/all_to_all | solution.py:356
  232.2 6.2 copy-start.46
  248.1 70.9 %all-to-all-start.4 = ((f32[8,128,128]{2,1,0:T(8,128)}), f32[8,128,128]{2,1,0:T(8,128)}, u32[]{:S(2)}, u32[]{:S(2)}) async-start(f32[8,128,128]{2,1,0:T(8,128)} %bitcast.533), calls=%async_computation.4 | async-start | bytes 1048576 | tf_op jit(solution)/shard_map/all_to_all | solution.py:375
  304.4 6.1 copy-start.14
  304.4 6.1 copy-start.58
  319.0 191.1 %all-to-all-start.2 = ((f32[8,128,256]{2,1,0:T(8,128)}), f32[8,128,256]{2,1,0:T(8,128)}, u32[]{:S(2)}, u32[]{:S(2)}) async-start(f32[8,128,256]{2,1,0:T(8,128)} %copy.183), calls=%async_computation.2 | async-start | bytes 2097152 | tf_op jit(solution)/shard_map/all_to_all | solution.py:356
  495.5 6.1 copy-start.56
  495.5 6.1 copy-start.59
  495.5 6.1 copy-start.65
  495.5 6.1 copy-start.70
  495.5 6.1 copy-start.75
  495.6 6.1 copy-start.79
  495.6 6.1 copy-start.83
  510.1 64.3 %all-to-all-start.5 = ((f32[8,128,256]{2,1,0:T(8,128)}), f32[8,128,256]{2,1,0:T(8,128)}, u32[]{:S(2)}, u32[]{:S(2)}) async-start(f32[8,128,256]{2,1,0:T(8,128)} %copy.210), calls=%async_computation.5 | async-start | bytes 2097152 | tf_op jit(solution)/shard_map/all_to_all | solution.py:356
  601.7 30.9 %all-to-all-start.6 = ((f32[8,128,128]{2,1,0:T(8,128)}), f32[8,128,128]{2,1,0:T(8,128)S(1)}, u32[]{:S(2)}, u32[]{:S(2)}) async-start(f32[8,128,128]{2,1,0:T(8,128)} %bitcast.197), calls=%async_computation.6 | async-start | bytes 1048576 | tf_op jit(solution)/shard_map/all_to_all | solution.py:375
  (68 other events, 157.5 us)
where the time goes:
time: 653 us; the launch traced here: 643 us
  Pallas kernels  276 us (42%)
  matrix products  121 us (19%)
  starting transfers between devices  66.7 us (10%)
  local copies, waits for them, and re-layouts  62.9 us (10%)
  waiting for transfers between devices  57.9 us (9%)
  other arithmetic  41.7 us (6%)
  between operations  17 us (3%)
    pallas_call x4, Pallas kernels, regular(): pl.pallas_call(body, out_shape=(jax.ShapeDtypeStruct((rows, columns), jnp...  212 us
    dot_general x28, matrix products, contract(): return jnp.einsum(form, left, right, precision=lax.Precision.HIGH)  121 us
    all_to_all x4, starting transfers between devices, forward(): lax.all_to_all(sent.reshape(groups, row_count, count * 2 * bins), 'gy', s...  55.3 us
    pallas_call x3, Pallas kernels, total(): pl.pallas_call(body, out_shape=jax.ShapeDtypeStruct((8, 128), jnp.float32...  51.6 us
    all_to_all x4, waiting for transfers between devices, forward(): lax.all_to_all(sent.reshape(groups, row_count, count * 2 * bins), 'gy', s...  32 us
    all_to_all x3, waiting for transfers between devices, inverse(): lax.all_to_all(sent, 'gy', split_axis=0, concat_axis=0, tiled=True)  25.9 us
  transfers between devices with their start and end apart: 7, of which 3 were waited for; matrix products, arithmetic and copies ran while one was open for 13% of the time, Pallas kernels for 35%

commit v1 on v0

--- a/solution.py
+++ b/solution.py
@@ -2,6 +2,7 @@
 
 import jax
 import jax.numpy as jnp
+import numpy as np
 from jax import lax
 from jax.experimental import pallas as pl
 from jax.experimental.pallas import tpu as pltpu
@@ -486,9 +487,1120 @@
     return (grad_measured, grad_stencil)
 
 
+def spectral_fits(mesh_y, mesh_z, planes, row_count, columns):
+    devices, rows, depth = (mesh_y * mesh_z, row_count * mesh_y, planes * mesh_z)
+    if columns % (16 * devices) or row_count % 128 or rows % 512 or planes != 1 or mesh_z % 2:
+        return False
+    tiles = 4 * depth // 8 * (rows // 128)
+    return depth < 8 and depth % 2 == 0 and devices % tiles == 0
+
+
+def wave_rows(length):
+    half, quarter = (length // 2, length // 4)
+    place = np.arange(half)[None, :]
+    tables = []
+    for odd in range(2):
+        frequency = 2 * np.arange(quarter)[:, None] + odd
+        angle = (place * frequency % length) * (2.0 * np.pi / length)
+        cosine, sine = (np.cos(angle), np.sin(angle))
+        if not odd:
+            sine[0] = np.cos(np.pi * place[0])
+        tables += [cosine, sine]
+    table = np.stack(tables)
+    high = table.astype(jnp.bfloat16)
+    low = (table - high.astype(np.float64)).astype(jnp.bfloat16)
+    return (high, low)
+
+
+def basis(length, place):
+    half = length // 2
+    frequency = np.concatenate([np.arange(0, half, 2), np.arange(1, half, 2)])
+    angle = frequency * place % length * (2.0 * np.pi / length)
+    cosine, sine = (np.cos(angle), np.sin(angle))
+    sine[0] = np.cos(np.pi * place)
+    return (cosine, sine)
+
+
+def axis_values(length):
+    cosine, sine = basis(length, 1)
+    pure = sine.copy()
+    pure[0] = 0.0
+    other = cosine.copy()
+    other[0] = -1.0
+    weight = np.full(length // 2, 2.0)
+    weight[0] = 1.0
+    values = [(cosine, other), (pure, pure), basis(length, 0), basis(length, length - 1), (weight, weight)]
+    for place in (0, 1, length - 2, length - 1):
+        values.append(tuple(weight * part / length for part in basis(length, place)))
+    return np.stack([np.stack(pair) for pair in values]).astype(np.float32)
+
+
+COS, SIN, FIRST, LAST, WEIGHT, AT = range(6)
+
+
+def split(value):
+    high = value.astype(jnp.bfloat16)
+    return (high, (value - high.astype(jnp.float32)).astype(jnp.bfloat16))
+
+
+def product(left, right, contracting):
+    numbers = (contracting, ((), ()))
+
+    def one(a, b):
+        return lax.dot_general(a, b, numbers, preferred_element_type=jnp.float32)
+
+    return one(left[0], right[0]) + (one(left[0], right[1]) + one(left[1], right[0]))
+
+
+class Spectral:
+    def __init__(self, count_y, count_z, planes, row_count, columns):
+        self.ny, self.nz = (count_y, count_z)
+        self.nd = count_y * count_z
+        self.depth = planes * count_z
+        self.row_count = row_count
+        self.rows = row_count * count_y
+        self.columns = columns
+        self.bins = columns // 2 // self.nd
+        self.half = self.rows // 2
+        self.steps = self.half // 128
+        self.tiers = self.bins // 8
+        self.lanes = self.rows // 128
+        self.tiles = 4 * self.depth // 8 * self.lanes
+        self.stride = self.nd // self.tiles
+
+    def place_of(self, index):
+        return (lax.rem(index, self.ny), lax.div(index, self.ny))
+
+    def scratch(self):
+        Z, bins, half, nd = (self.depth, self.bins, self.half, self.nd)
+        packed = (Z, 2, bins, self.rows)
+        field = (Z, 4, bins, half)
+        edge = (2, Z, 2, bins, 128)
+        F = jnp.float32
+        D = pltpu.SemaphoreType.DMA
+        names = dict(
+            sent_m=pltpu.VMEM((nd, 2, bins, 128 * (self.row_count // 128)), F),
+            sent_u=pltpu.VMEM((nd, 2, bins, self.row_count), F),
+            sent_p=pltpu.VMEM((self.ny, 2, bins, self.row_count), F),
+            got_m=pltpu.VMEM(packed, F),
+            got_u=pltpu.VMEM(packed, F),
+            got_p=pltpu.VMEM((2, bins, self.rows), F),
+            wave=pltpu.VMEM(packed, F),
+            wave_p=pltpu.VMEM((2, bins, self.rows), F),
+            v0=pltpu.VMEM(field, F),
+            v1=pltpu.VMEM(field, F),
+            v2=pltpu.VMEM(field, F),
+            up=pltpu.VMEM(field, F),
+            w3=pltpu.VMEM(field, F),
+            m0=pltpu.VMEM(field, F),
+            m1=pltpu.VMEM(field, F),
+            mw=pltpu.VMEM(field, F),
+            stencil=pltpu.VMEM((3, 2, 3, bins, half), F),
+            blur=pltpu.VMEM((2, 3, bins, half), F),
+            gain=pltpu.VMEM((2, 2, bins, half), F),
+            across=pltpu.VMEM((9, 2, bins, 128), F),
+            rows_v0=pltpu.VMEM(edge, F),
+            rows_v1=pltpu.VMEM(edge, F),
+            rows_v2=pltpu.VMEM(edge, F),
+            rows_up=pltpu.VMEM(edge, F),
+            rows_w3=pltpu.VMEM(edge, F),
+            rows_m0=pltpu.VMEM(edge, F),
+            rows_m1=pltpu.VMEM(edge, F),
+            rows_mw=pltpu.VMEM(edge, F),
+            edge_rows=pltpu.VMEM(edge, F),
+            cols_v0=pltpu.VMEM((4, 8, self.rows), F),
+            cols_v1=pltpu.VMEM((4, 8, self.rows), F),
+            cols_v2=pltpu.VMEM((4, 8, self.rows), F),
+            cols_up=pltpu.VMEM((4, 8, self.rows), F),
+            cols_w3=pltpu.VMEM((4, 8, self.rows), F),
+            cols_m0=pltpu.VMEM((2, 8, self.rows), F),
+            cols_m1=pltpu.VMEM((2, 8, self.rows), F),
+            cols_mw=pltpu.VMEM((2, 8, self.rows), F),
+            edge_cols=pltpu.VMEM((2, 8, self.rows), F),
+            part=pltpu.VMEM((3, 3, self.tiles, 8, 128), F),
+            slots=pltpu.VMEM((3, 3, nd, 8, 128), F),
+            sums=pltpu.VMEM((3, 3, 8, 128), F),
+            full=pltpu.VMEM((3, 3, self.tiles, 8, 128), F),
+            acc=pltpu.VMEM((8, 8, 128), F),
+            total=pltpu.VMEM((2, 8, 8, 128), F),
+            taps=pltpu.VMEM((27, 8, 128), F),
+            tap_part=pltpu.VMEM((8, 128), F),
+            tap_slots=pltpu.VMEM((nd, 8, 128), F),
+            sent_o=pltpu.VMEM(packed, F),
+            got_o=pltpu.VMEM((nd, 2, bins, self.row_count), F),
+            send_big=D((2, nd)),
+            recv_big=D((2, nd)),
+            send_p=D((self.ny,)),
+            recv_p=D((self.ny,)),
+            send_part=D((2, 3, self.tiles)),
+            recv_part=D((2, 3, nd)),
+            send_full=D((2, 3, nd)),
+            recv_full=D((2, 3, self.tiles)),
+            send_tap=D((nd,)),
+            recv_tap=D((nd,)),
+        )
+        return names
+
+
+    def remote(self, source, target, send, receive, peer):
+        return pltpu.make_async_remote_copy(
+            src_ref=source, dst_ref=target, send_sem=send, recv_sem=receive,
+            device_id=self.place_of(peer), device_id_type=MESH,
+        )
+
+    def spread_copy(self, r, sent, got, lot, peer, source):
+        y, z = self.place_of(source)
+        lanes = pl.ds(pl.multiple_of(y * self.row_count, 128), self.row_count)
+        return self.remote(
+            sent.at[peer], got.at[z, :, :, lanes], r.send_big.at[lot, peer], r.recv_big.at[lot, source], peer
+        )
+
+    def spread_start(self, r, sent, got, lot):
+        @pl.loop(1, self.nd)
+        def _(k):
+            peer = lax.rem(self.me + k, self.nd)
+            self.spread_copy(r, sent, got, lot, peer, self.me).start()
+
+        y, z = self.place_of(self.me)
+        lanes = pl.ds(pl.multiple_of(y * self.row_count, 128), self.row_count)
+        got[z, :, :, lanes] = sent[self.me]
+
+    def spread_wait(self, r, sent, got, lot):
+        @pl.loop(1, self.nd)
+        def _(k):
+            peer = lax.rem(self.me + k, self.nd)
+            copy = self.spread_copy(r, sent, got, lot, peer, peer)
+            copy.wait_recv()
+
+        @pl.loop(1, self.nd)
+        def _(k):
+            peer = lax.rem(self.me + k, self.nd)
+            self.spread_copy(r, sent, got, lot, peer, self.me).wait_send()
+
+    def point_copy(self, r, peer_y, source_y):
+        lanes = pl.ds(pl.multiple_of(source_y * self.row_count, 128), self.row_count)
+        return self.remote(
+            r.sent_p.at[peer_y], r.got_p.at[:, :, lanes], r.send_p.at[peer_y], r.recv_p.at[source_y],
+            self.z * self.ny + peer_y,
+        )
+
+    def point_start(self, r):
+        @pl.loop(1, self.ny)
+        def _(k):
+            self.point_copy(r, lax.rem(self.y + k, self.ny), self.y).start()
+
+        lanes = pl.ds(pl.multiple_of(self.y * self.row_count, 128), self.row_count)
+        r.got_p[:, :, lanes] = r.sent_p[self.y]
+
+    def point_wait(self, r):
+        @pl.loop(1, self.ny)
+        def _(k):
+            peer = lax.rem(self.y + k, self.ny)
+            self.point_copy(r, peer, peer).wait_recv()
+
+        @pl.loop(1, self.ny)
+        def _(k):
+            peer = lax.rem(self.y + k, self.ny)
+            self.point_copy(r, peer, self.y).wait_send()
+
+    def return_copy(self, r, peer, source):
+        y, z = self.place_of(peer)
+        lanes = pl.ds(pl.multiple_of(y * self.row_count, 128), self.row_count)
+        return self.remote(
+            r.sent_o.at[z, :, :, lanes], r.got_o.at[source], r.send_big.at[0, peer], r.recv_big.at[0, source], peer
+        )
+
+    def owner(self, kind, tile):
+        if kind == 0:
+            return tile * self.stride
+        if kind == 1:
+            return tile * self.stride + self.stride - 1
+        return self.nd - 1
+
+    def owned(self, kind):
+        if kind == 0:
+            return lax.rem(self.me, self.stride) == 0
+        if kind == 1:
+            return lax.rem(self.me, self.stride) == self.stride - 1
+        return self.me == self.nd - 1
+
+    def counts(self, kind):
+        return 1 if kind == 2 else self.tiles
+
+    def mine(self, kind):
+        return 0 if kind == 2 else lax.div(self.me, self.stride)
+
+    def reduce_start(self, r, turn, kinds):
+        lot = turn % 2
+        for kind in kinds:
+
+            @pl.loop(0, self.counts(kind))
+            def _(tile):
+                owner = self.owner(kind, tile)
+
+                @pl.when(owner != self.me)
+                def _():
+                    self.remote(
+                        r.part.at[turn, kind, tile], r.slots.at[turn, kind, self.me],
+                        r.send_part.at[lot, kind, tile], r.recv_part.at[lot, kind, self.me], owner,
+                    ).start()
+
+    def reduce_finish(self, r, turn, kinds):
+        lot = turn % 2
+        for kind in kinds:
+
+            @pl.when(self.owned(kind))
+            def _():
+                tile = self.mine(kind)
+                r.slots[turn, kind, self.me] = r.part[turn, kind, tile]
+
+                @pl.loop(1, self.nd)
+                def _(k):
+                    peer = lax.rem(self.me + k, self.nd)
+                    self.remote(
+                        r.part.at[turn, kind, tile], r.slots.at[turn, kind, peer],
+                        r.send_part.at[lot, kind, tile], r.recv_part.at[lot, kind, peer], peer,
+                    ).wait_recv()
+
+                lots = [r.slots[turn, kind, k] for k in range(self.nd)]
+                while len(lots) > 1:
+                    lots = [lots[k] + lots[k + 1] for k in range(0, len(lots) - 1, 2)] + lots[len(lots) // 2 * 2 :]
+                r.sums[turn, kind] = lots[0]
+
+                @pl.loop(1, self.nd)
+                def _(k):
+                    peer = lax.rem(self.me + k, self.nd)
+                    self.remote(
+                        r.sums.at[turn, kind], r.full.at[turn, kind, tile],
+                        r.send_full.at[lot, kind, peer], r.recv_full.at[lot, kind, tile], peer,
+                    ).start()
+
+                r.full[turn, kind, tile] = r.sums[turn, kind]
+
+        for kind in kinds:
+
+            @pl.loop(0, self.counts(kind))
+            def _(tile):
+                owner = self.owner(kind, tile)
+
+                @pl.when(owner != self.me)
+                def _():
+                    self.remote(
+                        r.sums.at[turn, kind], r.full.at[turn, kind, tile],
+                        r.send_full.at[lot, kind, owner], r.recv_full.at[lot, kind, tile], owner,
+                    ).wait_recv()
+                    self.remote(
+                        r.part.at[turn, kind, tile], r.slots.at[turn, kind, self.me],
+                        r.send_part.at[lot, kind, tile], r.recv_part.at[lot, kind, self.me], owner,
+                    ).wait_send()
+
+            @pl.when(self.owned(kind))
+            def _():
+                tile = self.mine(kind)
+
+                @pl.loop(1, self.nd)
+                def _(k):
+                    peer = lax.rem(self.me + k, self.nd)
+                    self.remote(
+                        r.sums.at[turn, kind], r.full.at[turn, kind, tile],
+                        r.send_full.at[lot, kind, peer], r.recv_full.at[lot, kind, tile], peer,
+                    ).wait_send()
+
+
+    def row_spectra(self, r, source, sent):
+        half = self.columns // 2
+        low, high = (source[:, :half], source[:, half:])
+        per = self.nd // 2
+        for odd, value in enumerate((low + high, low - high)):
+            value = split(value)
+            for part in range(2):
+                table = (r.tab_x[0][2 * odd + part], r.tab_x[1][2 * odd + part])
+                sent[pl.ds(odd * per, per), part] = product(table, value, ((1,), (1,))).reshape(
+                    per, self.bins, self.row_count
+                )
+
+    def point_spectra(self, r, source):
+        half = self.columns // 2
+        low, high = (source[:, :half], source[:, half:])
+        odd = lax.div(2 * self.z, self.nz)
+        sign = 1.0 - 2.0 * odd.astype(jnp.float32)
+        value = split(low + sign * high)
+        block = self.ny * self.bins
+        start = pl.multiple_of(lax.rem(self.z, self.nz // 2) * block, block)
+        for part in range(2):
+            table = tuple(half_table[2 * odd + part, pl.ds(start, block)] for half_table in r.tab_x)
+            r.sent_p[:, part] = product(table, value, ((1,), (1,))).reshape(self.ny, self.bins, self.row_count)
+
+    def column_spectra(self, r, got, wave):
+        count = math.prod(got.shape[:-1])
+        value = got[...].reshape(count, self.rows)
+        low, high = (value[:, : self.half], value[:, self.half :])
+        quarter = self.half // 2
+        for odd, value in enumerate((low + high, low - high)):
+            value = split(value)
+            for part in range(2):
+                table = (r.tab_y[0][2 * odd + part], r.tab_y[1][2 * odd + part])
+                wave[..., pl.ds(part * self.half + odd * quarter, quarter)] = product(
+                    value, table, ((1,), (1,))
+                ).reshape(got.shape[:-1] + (quarter,))
+
+    def column_values(self, r, wave, target):
+        count = math.prod(wave.shape[:-1])
+        value = wave[...].reshape(count, self.rows)
+        quarter = self.half // 2
+        even, odd = (
+            sum(
+                product(
+                    split(value[:, part * self.half + k * quarter : part * self.half + (k + 1) * quarter]),
+                    (r.tab_y[0][2 * k + part], r.tab_y[1][2 * k + part]),
+                    ((1,), (0,)),
+                )
+                for part in range(2)
+            )
+            for k in range(2)
+        )
+        shape = wave.shape[:-1] + (self.half,)
+        target[..., : self.half] = (even + odd).reshape(shape)
+        target[..., self.half :] = (even - odd).reshape(shape)
+
+    def row_values(self, r, got, out):
+        per = self.nd // 2
+        sides = []
+        for k in range(2):
+            side = 0.0
+            for part in range(2):
+                value = got[pl.ds(k * per, per), part].reshape(per * self.bins, self.row_count)
+                side = side + product(
+                    split(value.T), (r.tab_x[0][2 * k + part], r.tab_x[1][2 * k + part]), ((1,), (0,))
+                )
+            sides.append(side)
+        half = self.columns // 2
+        out[0, :, :half] = sides[0] + sides[1]
+        out[0, :, half:] = sides[0] - sides[1]
+
+
+    def masks(self, tier, step):
+        shape = (8, 128)
+        row = (lax.broadcasted_iota(jnp.int32, shape, 0) == 0) & (self.me == 0)
+        lane = lax.broadcasted_iota(jnp.int32, shape, 1) + 128 * step == 0
+        if tier:
+            row = row & False
+        return (row, lane, row & lane, row | lane)
+
+    def combine(self, masks, ac, as_, bc, bs):
+        row, lane, corner, special = masks
+        pr = jnp.where(special, ac, ac - bs)
+        pi = jnp.where(corner, as_, jnp.where(row, -as_, jnp.where(lane, -bc, -(as_ + bc))))
+        mr = jnp.where(row, bc, jnp.where(lane, as_, ac + bs))
+        mi = jnp.where(corner, bs, jnp.where(special, -bs, as_ - bc))
+        return [pr, pi, mr, mi]
+
+    def separate(self, masks, field):
+        row, lane, corner, special = masks
+        pr, pi, mr, mi = field
+        ac = jnp.where(special, pr, 0.5 * (pr + mr))
+        as_ = jnp.where(corner, pi, jnp.where(row, -pi, jnp.where(lane, mr, 0.5 * (mi - pi))))
+        bc = jnp.where(row, mr, jnp.where(lane, -pi, -0.5 * (pi + mi)))
+        bs = jnp.where(corner, mi, jnp.where(special, -mi, 0.5 * (mr - pr)))
+        return (ac, as_, bc, bs)
+
+    def lane_slice(self, step, part=0):
+        return pl.ds(pl.multiple_of(part * self.half + step * 128, 128), 128)
+
+    def along(self, r, which, step, part):
+        return r.along[which, :, self.lane_slice(step, part)]
+
+    def beside(self, r, which, part, tier):
+        return r.across[which, part, pl.ds(8 * tier, 8)]
+
+    def load(self, field, z, tier, step):
+        return [field[z, k, pl.ds(8 * tier, 8), self.lane_slice(step)] for k in range(4)]
+
+    def keep(self, field, z, tier, step, values):
+        for k in range(4):
+            field[z, k, pl.ds(8 * tier, 8), self.lane_slice(step)] = values[k]
+
+    def load_wave(self, wave, z, tier, step):
+        return [
+            wave[z, part, pl.ds(8 * tier, 8), self.lane_slice(step, side)]
+            for part in range(2)
+            for side in range(2)
+        ]
+
+    def times(self, factor, value, conjugate=False):
+        out = []
+        for side in range(2):
+            real, other, cross = factor[side]
+            a, b = (value[2 * side], value[2 * side + 1])
+            if conjugate:
+                out += [real * a + cross * b, other * b - cross * a]
+            else:
+                out += [real * a - cross * b, other * b + cross * a]
+        return out
+
+    def factor(self, array, tier, step):
+        where = (pl.ds(8 * tier, 8), self.lane_slice(step))
+        return [[array[(side, k) + where] for k in range(3)] for side in range(2)]
+
+    def sweep(self, body):
+        @pl.loop(0, self.steps)
+        def _(step):
+            columns = {}
+            for tier in range(self.tiers):
+                body(tier, step, self.masks(tier, step), columns)
+
+    def frames(self, r, masks, tier, step, z, value, rows, columns=None):
+        ac, as_, bc, bs = self.separate(masks, value)
+        here = pl.ds(8 * tier, 8)
+        for k, which in enumerate((AT, AT + 3)):
+            c, s = (self.along(r, which, step, 0), self.along(r, which, step, 1))
+            rows[k, z, 0, here] += ac * c + as_ * s
+            rows[k, z, 1, here] += bc * c + bs * s
+        if columns is None:
+            return
+        for x in range(4):
+            a, b = (self.beside(r, AT + x, 0, tier), self.beside(r, AT + x, 1, tier))
+            for side, (p, q) in enumerate(((ac, bc), (as_, bs))):
+                term = a * p + b * q
+                key = (x, z, side)
+                columns[key] = term if key not in columns else columns[key] + term
+
+    def put_columns(self, part, tier, step, columns):
+        if tier < self.tiers - 1:
+            return
+        for (x, z, side), value in columns.items():
+            index = x * self.depth + z
+            tile = index // 8 * self.lanes + side * self.steps + step
+            part[tile, pl.ds(index % 8, 1)] = jnp.sum(value, 0, keepdims=True)
+
+    def clear(self, *refs):
+        for ref in refs:
+            ref[...] = jnp.zeros(ref.shape, jnp.float32)
+
+    def settle(self, rows):
+        for k in range(2):
+            rows[k] = jnp.broadcast_to(jnp.sum(rows[k], -1, keepdims=True), rows.shape[1:])
+
+    def unpack(self, full, cols):
+        Z = self.depth
+        cols[...] = jnp.zeros(cols.shape, jnp.float32)
+        for x in range(4):
+            first = x * Z
+            for lane in range(self.lanes):
+                cols[x, pl.ds(0, Z), pl.ds(lane * 128, 128)] = full[
+                    first // 8 * self.lanes + lane, pl.ds(first % 8, Z)
+                ]
+
+    def shifted(self, value, by):
+        if by == 0:
+            return value
+        value = pltpu.roll(value, 7 if by > 0 else 1, 0)
+        sub = lax.broadcasted_iota(jnp.int32, value.shape, 0)
+        return jnp.where(sub < self.depth, value, 0.0)
+
+    def corners(self, r, col):
+        out = []
+        for which in (AT, AT + 3):
+            weight = jnp.concatenate([r.along[which, :, :]], 0)
+            out.append(jnp.broadcast_to(jnp.sum(col * weight, -1, keepdims=True), (8, 128)))
+        return out
+
+    def edges(self, r, w, rows, col_first, col_last, inner=None, mapped=None):
+        Z = self.depth
+        k_first, k_last = (self.corners(r, col_first[...]), self.corners(r, col_last[...]))
+        total = lambda terms: sum(terms[1:], terms[0])
+        q = {}
+        for name, b, c, value in ((0, 0, 0, k_last[1]), (1, 0, 2, k_first[1]), (2, 2, 0, k_last[0]), (3, 2, 2, k_first[0])):
+            q[name] = total([w(a, b, c) * self.shifted(value, a - 1) for a in range(3)])
+        if inner is not None:
+            near, far = inner
+            k_near, k_far = (self.corners(r, near[...]), self.corners(r, far[...]))
+            fix = []
+            for (c0, v0), (c1, v1) in (((1, k_first), (2, k_near)), ((0, k_far), (1, k_last))):
+                fix.append(
+                    [
+                        total(
+                            [
+                                w(a, b, c0) * self.shifted(v0[y], a - 1) + w(a, b, c1) * self.shifted(v1[y], a - 1)
+                                for a in range(3)
+                            ]
+                        )
+                        for b, y in ((0, 1), (2, 0))
+                    ]
+                )
+
+        @pl.loop(0, self.steps)
+        def _(step):
+            c = [self.along(r, COS, step, part) for part in range(2)]
+            s = self.along(r, SIN, step, 0)
+            first = [self.along(r, FIRST, step, part) for part in range(2)]
+            last = [self.along(r, LAST, step, part) for part in range(2)]
+
+            def get(col):
+                return [col[:, self.lane_slice(step, part)] for part in range(2)]
+
+            def line(a, c_index, col):
+                w0, w1, w2 = (w(a, b, c_index) for b in range(3))
+                turn = (w2 - w0) * s
+                return [
+                    (w1 + (w0 + w2) * c[0]) * col[0] + turn * col[1],
+                    (w1 + (w0 + w2) * c[1]) * col[1] - turn * col[0],
+                ]
+
+            def stacked(pieces):
+                out = None
+                for a in range(3):
+                    for c_index, col in pieces:
+                        term = [self.shifted(part, a - 1) for part in line(a, c_index, col)]
+                        out = term if out is None else [p + t for p, t in zip(out, term)]
+                return out
+
+            f, l = (get(col_first), get(col_last))
+            for k, (pieces, upper, lower) in enumerate((([(0, l)], q[0], q[2]), ([(2, f)], q[1], q[3]))):
+                value = stacked(pieces)
+                for part in range(2):
+                    r.edge_cols[k, :, self.lane_slice(step, part)] = (
+                        value[part] - upper * first[part] - lower * last[part]
+                    )
+            if inner is not None:
+                n, g = (get(near), get(far))
+                for k, pieces in enumerate(([(1, f), (2, n)], [(0, g), (1, l)])):
+                    value = stacked(pieces)
+                    for part in range(2):
+                        mapped[k, :, self.lane_slice(step, part)] = (
+                            value[part] - fix[k][0] * first[part] - fix[k][1] * last[part]
+                        )
+
+        for tier in range(self.tiers):
+            here = pl.ds(8 * tier, 8)
+            c = [self.beside(r, COS, part, tier) for part in range(2)]
+            s = self.beside(r, SIN, 0, tier)
+            for k, (b, source) in enumerate(((0, 1), (2, 0))):
+                for z in range(Z):
+                    out = None
+                    for a in range(3):
+                        if not 0 <= z + a - 1 < Z:
+                            continue
+                        w0, w1, w2 = (w(a, b, c_index) for c_index in range(3))
+                        turn = (w2 - w0) * s
+                        p, t = (rows[source, z + a - 1, part, here] for part in range(2))
+                        term = [
+                            (w1 + (w0 + w2) * c[0]) * p + turn * t,
+                            (w1 + (w0 + w2) * c[1]) * t - turn * p,
+                        ]
+                        out = term if out is None else [x + v for x, v in zip(out, term)]
+                    for part in range(2):
+                        r.edge_rows[k, z, part, here] = out[part]
+
+    def edge_field(self, r, masks, tier, step, z):
+        here = pl.ds(8 * tier, 8)
+        out = []
+        for part in range(2):
+            e0, e1 = (r.edge_rows[k, z, part, here] for k in range(2))
+            x0, x1 = (self.beside(r, which, part, tier) for which in (FIRST, LAST))
+            for side in range(2):
+                y0, y1 = (self.along(r, which, step, side) for which in (FIRST, LAST))
+                c0, c1 = (r.edge_cols[k, pl.ds(z, 1), self.lane_slice(step, side)] for k in range(2))
+                out.append(e0 * y0 + e1 * y1 + x0 * c0 + x1 * c1)
+        return self.combine(masks, *out)
+
+    def stencil_field(self, r, masks, tier, step, field, flip):
+        Z = self.depth
+        value = [self.load(field, z, tier, step) for z in range(Z)]
+        out = [[-e for e in self.edge_field(r, masks, tier, step, z)] for z in range(Z)]
+        for a in range(3):
+            where = (pl.ds(8 * tier, 8), self.lane_slice(step))
+            factor = [[r.stencil[(a, side, k) + where] for k in range(3)] for side in range(2)]
+            for z in range(Z):
+                other = z + (1 - a if flip else a - 1)
+                if 0 <= other < Z:
+                    term = self.times(factor, value[other], flip)
+                    out[z] = [o + t for o, t in zip(out[z], term)]
+        return out
+
+    def build_stencil(self, r, w):
+        def body(tier, step, masks, columns):
+            row, lane, corner, special = masks
+            here = pl.ds(8 * tier, 8)
+            sx = self.beside(r, SIN, 0, tier)
+            ys = self.along(r, SIN, step, 0)
+            for side in range(2):
+                cx = self.beside(r, COS, side, tier)
+                cy = self.along(r, COS, step, 0)
+                sy = jnp.broadcast_to(ys, (8, 128))
+                cy = jnp.broadcast_to(cy, (8, 128))
+                if side:
+                    cy = jnp.where(row, cy, self.along(r, COS, step, 1))
+                    sy = jnp.where(row, sy, -sy)
+                for a in range(3):
+                    real, imag = ([], [])
+                    for b in range(3):
+                        real.append(w(a, b, 1) + (w(a, b, 0) + w(a, b, 2)) * cx)
+                        imag.append((w(a, b, 2) - w(a, b, 0)) * sx)
+                    value = real[1] + (real[0] + real[2]) * cy - (imag[2] - imag[0]) * sy
+                    cross = imag[1] + (imag[0] + imag[2]) * cy + (real[2] - real[0]) * sy
+                    other = jnp.where(corner, real[1] - (real[0] + real[2]), value)
+                    for k, item in enumerate((value, other, cross)):
+                        r.stencil[a, side, k, here, self.lane_slice(step)] = item
+
+        self.sweep(body)
+
+    def build_blur(self, r):
+        def body(tier, step, masks, columns):
+            row, lane, corner, special = masks
+            here = pl.ds(8 * tier, 8)
+            wave = [
+                r.wave_p[part, here, self.lane_slice(step, side)] for part in range(2) for side in range(2)
+            ]
+            value = self.combine(masks, wave[0], wave[1], wave[2], wave[3])
+            for side in range(2):
+                real, imag = (value[2 * side], value[2 * side + 1])
+                other = jnp.where(corner, imag, real)
+                cross = jnp.where(corner, 0.0, imag)
+                for k, item in enumerate((real, other, cross)):
+                    r.blur[side, k, here, self.lane_slice(step)] = item
+                square = cross * cross
+                r.gain[side, 0, here, self.lane_slice(step)] = real * real + square
+                r.gain[side, 1, here, self.lane_slice(step)] = other * other + square
+
+        self.sweep(body)
+
+    def gained(self, r, tier, step, value):
+        where = (pl.ds(8 * tier, 8), self.lane_slice(step))
+        return [r.gain[(k // 2, k % 2) + where] * value[k] for k in range(4)]
+
+    def dot(self, masks, left, right):
+        corner = masks[2]
+        total = sum(a * b for a, b in zip(left, right))
+        return jnp.where(corner, 0.5 * total, total)
+
+
+    def stencil_twice(self, r, w, field, rows, cols, mapped, rows_m, cols_m, finish, after=None):
+        def flipped(a, b, c):
+            return w(2 - a, 2 - b, 2 - c)
+
+        self.edges(r, w, rows, cols.at[0], cols.at[3], (cols.at[1], cols.at[2]), cols_m)
+        self.clear(rows_m)
+
+        def forward(tier, step, masks, columns):
+            out = self.stencil_field(r, masks, tier, step, field, False)
+            for z in range(self.depth):
+                self.keep(mapped, z, tier, step, out[z])
+                self.frames(r, masks, tier, step, z, out[z], rows_m)
+
+        self.sweep(forward)
+        self.settle(rows_m)
+        self.edges(r, flipped, rows_m, cols_m.at[0], cols_m.at[1])
+
+        def back(tier, step, masks, columns):
+            finish(tier, step, masks, columns, self.stencil_field(r, masks, tier, step, mapped, True))
+
+        self.sweep(back)
+
+    def scalars_out(self, r, turn, count):
+        for k in range(count):
+            r.part[turn, 2, 0, pl.ds(k, 1)] = jnp.sum(r.acc[k], 0, keepdims=True)
+        for k in range(count, 8):
+            r.part[turn, 2, 0, pl.ds(k, 1)] = jnp.zeros((1, 128), jnp.float32)
+
+    def scalars_in(self, r, turn, count):
+        value = jnp.sum(r.full[turn, 2, 0], -1, keepdims=True)
+        return [jnp.broadcast_to(value[k : k + 1], (8, 128)) for k in range(count)]
+
+    def run(self, r):
+        Z = self.depth
+        self.y, self.z = (lax.axis_index("gy"), lax.axis_index("gz"))
+        self.me = self.z * self.ny + self.y
+
+        def w(a, b, c):
+            return r.weights[9 * a + 3 * b + c]
+
+        barrier = pltpu.get_barrier_semaphore()
+
+        @pl.loop(1, self.nd)
+        def _(k):
+            pl.semaphore_signal(
+                barrier, inc=1, device_id=self.place_of(lax.rem(self.me + k, self.nd)), device_id_type=MESH
+            )
+
+        own = r.frequencies[self.me]
+        for which in range(9):
+            for part in range(2):
+                r.across[which, part] = jnp.broadcast_to(
+                    own[part * self.bins : (part + 1) * self.bins, which : which + 1], (self.bins, 128)
+                )
+        self.point_spectra(r, r.point_spread[...])
+        self.row_spectra(r, r.measured[0], r.sent_m)
+        pl.semaphore_wait(barrier, self.nd - 1)
+        self.point_start(r)
+        self.spread_start(r, r.sent_m, r.got_m, 0)
+        self.row_spectra(r, r.upstream[0], r.sent_u)
+        self.spread_start(r, r.sent_u, r.got_u, 1)
+        self.build_stencil(r, w)
+        self.clear(r.rows_v0, r.rows_v1, r.rows_v2, r.rows_up, r.acc, r.taps)
+
+        self.point_wait(r)
+        self.column_spectra(r, r.got_p, r.wave_p)
+        self.build_blur(r)
+        self.spread_wait(r, r.sent_m, r.got_m, 0)
+        self.column_spectra(r, r.got_m, r.wave)
+
+        def start(tier, step, masks, columns):
+            factor = self.factor(r.blur, tier, step)
+            for z in range(Z):
+                value = self.combine(masks, *self.load_wave(r.wave, z, tier, step))
+                value = self.times(factor, value, True)
+                self.keep(r.v0, z, tier, step, value)
+                self.frames(r, masks, tier, step, z, value, r.rows_v0, columns)
+            self.put_columns(r.part.at[0, 0], tier, step, columns)
+
+        self.sweep(start)
+        self.reduce_start(r, 0, [0])
+        self.settle(r.rows_v0)
+        self.reduce_finish(r, 0, [0])
+        self.unpack(r.full.at[0, 0], r.cols_v0)
+
+        def first(tier, step, masks, columns, back):
+            for z in range(Z):
+                before = self.load(r.v0, z, tier, step)
+                value = [g + b for g, b in zip(self.gained(r, tier, step, before), back[z])]
+                self.keep(r.v1, z, tier, step, value)
+                self.frames(r, masks, tier, step, z, value, r.rows_v1, columns)
+                r.acc[0] += self.dot(masks, before, before)
+                r.acc[1] += self.dot(masks, before, value)
+                r.acc[2] += self.dot(masks, value, value)
+            self.put_columns(r.part.at[1, 0], tier, step, columns)
+
+        self.stencil_twice(r, w, r.v0, r.rows_v0, r.cols_v0, r.m0, r.rows_m0, r.cols_m0, first)
+        self.scalars_out(r, 1, 3)
+        self.reduce_start(r, 1, [0, 2])
+        self.settle(r.rows_v1)
+        self.spread_wait(r, r.sent_u, r.got_u, 1)
+        self.column_spectra(r, r.got_u, r.wave)
+
+        def upper(tier, step, masks, columns):
+            for z in range(Z):
+                value = self.combine(masks, *self.load_wave(r.wave, z, tier, step))
+                self.keep(r.up, z, tier, step, value)
+                self.frames(r, masks, tier, step, z, value, r.rows_up, columns)
+            self.put_columns(r.part.at[2, 1], tier, step, columns)
+
+        self.sweep(upper)
+        self.settle(r.rows_up)
+        self.clear(r.acc)
+        self.reduce_finish(r, 1, [0, 2])
+        self.reduce_start(r, 2, [1])
+        self.unpack(r.full.at[1, 0], r.cols_v1)
+        norm_0, curve_0, image_0 = self.scalars_in(r, 1, 3)
+        step_0 = norm_0 / curve_0
+
+        def second(tier, step, masks, columns, back):
+            for z in range(Z):
+                before, value = (self.load(f, z, tier, step) for f in (r.v0, r.v1))
+                up = self.load(r.up, z, tier, step)
+                after = [g + b for g, b in zip(self.gained(r, tier, step, value), back[z])]
+                self.keep(r.v2, z, tier, step, after)
+                self.frames(r, masks, tier, step, z, after, r.rows_v2, columns)
+                residual = [p - step_0 * q for p, q in zip(before, value)]
+                image = [p - step_0 * q for p, q in zip(value, after)]
+                for k, (p, q) in enumerate(
+                    ((residual, residual), (residual, value), (residual, image), (image, value), (up, residual), (up, before), (up, value))
+                ):
+                    r.acc[k] += self.dot(masks, p, q)
+            self.put_columns(r.part.at[2, 0], tier, step, columns)
+
+        self.stencil_twice(r, w, r.v1, r.rows_v1, r.cols_v1, r.m1, r.rows_m1, r.cols_m1, second)
+        self.scalars_out(r, 2, 7)
+        self.reduce_start(r, 2, [0, 2])
+        self.settle(r.rows_v2)
+        self.reduce_finish(r, 2, [0, 1, 2])
+        self.unpack(r.full.at[2, 0], r.cols_v2)
+        self.unpack(r.full.at[2, 1], r.cols_up)
+
+        norm_1, cross, inner, image_cross, up_residual, up_0, up_1 = self.scalars_in(r, 2, 7)
+        ratio = norm_1 / norm_0
+        curve_1 = inner + 2.0 * ratio * cross + ratio * ratio * curve_0
+        step_1 = norm_1 / curve_1
+        grad_step_1 = up_residual + ratio * up_0
+        grad_curve_1 = -grad_step_1 * step_1 / curve_1
+        grad_ratio = step_1 * up_0 + 2.0 * grad_curve_1 * (cross + ratio * curve_0)
+        grad_norm = grad_step_1 / curve_1 + grad_ratio / norm_0
+        grad_step_0 = (
+            up_0 - step_1 * up_1 - 2.0 * grad_curve_1 * (image_cross + ratio * image_0) - 2.0 * grad_norm * cross
+        )
+        more = 1.0 + ratio
+        g0 = grad_norm - grad_ratio * ratio / norm_0 + grad_step_0 / curve_0
+        g1 = grad_curve_1 * more * more - 2.0 * grad_norm * step_0 - grad_step_0 * step_0 / curve_0
+        g2 = -2.0 * grad_curve_1 * step_0 * more + grad_norm * step_0 * step_0
+        g3 = grad_curve_1 * step_0 * step_0
+        q0 = step_0 + step_1 * more
+        q1 = -step_1 * step_0
+        mix = (g1, 2.0 * g2, 2.0 * g3, q1)
+
+        def mixed(*values):
+            return mix[0] * values[0] + mix[1] * values[1] + mix[2] * values[2] + mix[3] * values[3]
+
+        for x in range(4):
+
+            @pl.loop(0, self.lanes)
+            def _(lane):
+                here = (x, slice(None), pl.ds(pl.multiple_of(lane * 128, 128), 128))
+                r.cols_w3[here] = mixed(*(f[here] for f in (r.cols_v0, r.cols_v1, r.cols_v2, r.cols_up)))
+
+        for k in range(2):
+            for part in range(2):
+                for tier in range(self.tiers):
+
+                    @pl.loop(0, Z)
+                    def _(z):
+                        here = (k, z, part, pl.ds(8 * tier, 8))
+                        r.rows_w3[here] = mixed(*(f[here] for f in (r.rows_v0, r.rows_v1, r.rows_v2, r.rows_up)))
+
+        def blend(tier, step, masks, columns):
+            for z in range(Z):
+                values = [self.load(f, z, tier, step) for f in (r.v0, r.v1, r.v2, r.up)]
+                self.keep(r.w3, z, tier, step, [mixed(*parts) for parts in zip(*values)])
+
+        self.sweep(blend)
+        scale = 1.0 / (self.rows * self.columns)
+
+        def last(tier, step, masks, columns, back):
+            factor = self.factor(r.blur, tier, step)
+            here = pl.ds(8 * tier, 8)
+            for z in range(Z):
+                v0, v1, w3, up = (self.load(f, z, tier, step) for f in (r.v0, r.v1, r.w3, r.up))
+                value = [
+                    b + d + 2.0 * g0 * p + g1 * q + q0 * u
+                    for b, d, p, q, u in zip(back[z], self.gained(r, tier, step, w3), v0, v1, up)
+                ]
+                value = self.separate(masks, self.times(factor, value))
+                for part in range(2):
+                    heavy = scale * self.beside(r, WEIGHT, part, tier)
+                    for side in range(2):
+                        r.wave[z, part, here, self.lane_slice(step, side)] = (
+                            value[2 * part + side] * heavy * self.along(r, WEIGHT, step, side)
+                        )
+
+        self.stencil_twice(r, w, r.w3, r.rows_w3, r.cols_w3, r.mw, r.rows_mw, r.cols_mw, last)
+        self.column_values(r, r.wave, r.sent_o)
+
+        @pl.loop(1, self.nd)
+        def _(k):
+            self.return_copy(r, lax.rem(self.me + k, self.nd), self.me).start()
+
+        lanes = pl.ds(pl.multiple_of(self.y * self.row_count, 128), self.row_count)
+        r.got_o[self.me] = r.sent_o[self.z, :, :, lanes]
+
+        self.tap_sums(r, 2.0 * g3)
+
+        @pl.loop(1, self.nd)
+        def _(k):
+            peer = lax.rem(self.me + k, self.nd)
+            self.remote(
+                r.tap_part, r.tap_slots.at[self.me], r.send_tap.at[peer], r.recv_tap.at[self.me], peer
+            ).start()
+
+        r.tap_slots[self.me] = r.tap_part[...]
+
+        @pl.loop(1, self.nd)
+        def _(k):
+            peer = lax.rem(self.me + k, self.nd)
+            self.return_copy(r, peer, peer).wait_recv()
+
+        self.row_values(r, r.got_o, r.out)
+
+        @pl.loop(1, self.nd)
+        def _(k):
+            peer = lax.rem(self.me + k, self.nd)
+            self.return_copy(r, peer, self.me).wait_send()
+            self.remote(
+                r.tap_part, r.tap_slots.at[peer], r.send_tap.at[peer], r.recv_tap.at[peer], peer
+            ).wait()
+
+        lots = [r.tap_slots[k] for k in range(self.nd)]
+        while len(lots) > 1:
+            lots = [lots[k] + lots[k + 1] for k in range(0, len(lots) - 1, 2)] + lots[len(lots) // 2 * 2 :]
+        r.tap_out[...] = lots[0] / math.sqrt(self.depth * self.rows * self.columns)
+
+    def tap_sums(self, r, weight):
+        Z = self.depth
+        pairs = ((r.v0, r.mw, None), (r.w3, r.m0, None), (r.v1, r.m1, weight))
+
+        def body(tier, step, masks, columns):
+            corner = masks[2]
+            sx = self.beside(r, SIN, 0, tier)
+            gamma = [[None, None, None, None] for a in range(3)]
+            for left, right, scale in pairs:
+                x = [self.load(left, z, tier, step) for z in range(Z)]
+                if scale is not None:
+                    x = [[scale * item for item in value] for value in x]
+                for z in range(Z):
+                    m = self.load(right, z, tier, step)
+                    for a in range(3):
+                        if not 0 <= z + a - 1 < Z:
+                            continue
+                        v = x[z + a - 1]
+                        for side in range(2):
+                            vr, vi, mr, mi = (v[2 * side], v[2 * side + 1], m[2 * side], m[2 * side + 1])
+                            p, q = (vr * mr, vi * mi)
+                            terms = (jnp.where(corner, 0.5 * (p + q), p + q), jnp.where(corner, 0.5 * (p - q), p + q), vi * mr - vr * mi)
+                            old = gamma[a][side]
+                            gamma[a][side] = terms if old is None else [o + t for o, t in zip(old, terms)]
+            for a in range(3):
+                sums = [0.0] * 9
+                for side in range(2):
+                    cx = self.beside(r, COS, side, tier)
+                    cy = jnp.broadcast_to(self.along(r, COS, step, 0), (8, 128))
+                    sy = jnp.broadcast_to(self.along(r, SIN, step, 0), (8, 128))
+                    if side:
+                        cy = jnp.where(masks[0], cy, self.along(r, COS, step, 1))
+                        sy = jnp.where(masks[0], sy, -sy)
+                    near, far, turn = gamma[a][side]
+                    items = (
+                        near, near * cx, far * cy, far * cy * cx, near * sx * sy,
+                        turn * sx, turn * sy, turn * cx * sy, turn * sx * cy,
+                    )
+                    sums = [s + item for s, item in zip(sums, items)]
+                for k in range(9):
+                    r.taps[9 * a + k] += sums[k]
+
+        self.sweep(body)
+
+        sides = (
+            (r.rows_v0, r.cols_v0, r.rows_mw, r.cols_mw, None),
+            (r.rows_w3, r.cols_w3, r.rows_m0, r.cols_m0, None),
+            (r.rows_v1, r.cols_v1, r.rows_m1, r.cols_m1, weight),
+        )
+        zero = jnp.zeros((8, 128), jnp.float32)
+        by_row = [[[zero] * 3 for k in range(2)] for a in range(3)]
+        by_col = [[[zero] * 3 for k in range(2)] for a in range(3)]
+        by_corner = [[[zero] * 2 for k in range(2)] for a in range(3)]
+        for rows_x, cols_x, rows_m, cols_m, scale in sides:
+            extra = 1.0 if scale is None else scale
+            for tier in range(self.tiers):
+                here = pl.ds(8 * tier, 8)
+                heavy = self.beside(r, WEIGHT, 0, tier) * extra
+                ca, cb = (self.beside(r, COS, part, tier) for part in range(2))
+                s = self.beside(r, SIN, 0, tier)
+                for k in range(2):
+                    for z in range(Z):
+                        ma, mb = (rows_m[k, z, part, here] for part in range(2))
+                        for a in range(3):
+                            if not 0 <= z + a - 1 < Z:
+                                continue
+                            xa, xb = (rows_x[1 - k, z + a - 1, part, here] for part in range(2))
+                            p, q = (heavy * xa * ma, heavy * xb * mb)
+                            terms = (p + q, p * ca + q * cb, heavy * s * (xa * mb - xb * ma))
+                            by_row[a][k] = [o + t for o, t in zip(by_row[a][k], terms)]
+            for k in range(2):
+                col_x, col_m = (cols_x.at[0 if k else 3], cols_m.at[k])
+                for step in range(self.steps):
+                    (xc, xs), (mc, ms) = (
+                        [ref[:, pl.ds(part * self.half + 128 * step, 128)] * (extra if ref is col_x else 1.0) for part in range(2)]
+                        for ref in (col_x, col_m)
+                    )
+                    heavy = self.along(r, WEIGHT, step, 0)
+                    cc, cs = (self.along(r, COS, step, part) for part in range(2))
+                    s = self.along(r, SIN, step, 0)
+                    for a in range(3):
+                        xc_a, xs_a = (self.shifted(item, a - 1) for item in (xc, xs))
+                        p, q = (heavy * xc_a * mc, heavy * xs_a * ms)
+                        terms = (p + q, p * cc + q * cs, heavy * s * (xc_a * ms - xs_a * mc))
+                        by_col[a][k] = [o + t for o, t in zip(by_col[a][k], terms)]
+                at_x, at_m = (self.corners(r, ref[...]) for ref in (col_x, col_m))
+                for a in range(3):
+                    for edge in range(2):
+                        term = extra * self.shifted(at_x[1 - edge], a - 1) * at_m[edge]
+                        by_corner[a][edge][k] = by_corner[a][edge][k] + term
+
+        lane = lax.broadcasted_iota(jnp.int32, (8, 128), 1)
+        lots = []
+        for a in range(3):
+            s = [r.taps[9 * a + k] for k in range(9)]
+            for b in range(3):
+                for c in range(3):
+                    beta, gamma = (float(b - 1), float(c - 1))
+                    if b == 1 and c == 1:
+                        value = s[0]
+                    elif b == 1:
+                        value = s[1] - gamma * s[5]
+                    elif c == 1:
+                        value = s[2] - beta * s[6]
+                    else:
+                        value = s[3] - beta * gamma * s[4] - beta * s[7] - gamma * s[8]
+                    value = value * (2.0 / (self.rows * self.columns))
+                    if b != 1:
+                        one, two, three = by_row[a][b // 2]
+                        value = value - (one if c == 1 else two - gamma * three) * (1.0 / (128 * self.columns))
+                    if c != 1:
+                        one, two, three = by_col[a][c // 2]
+                        value = value - (one if b == 1 else two - beta * three) * (1.0 / (self.rows * self.nd))
+                    if b != 1 and c != 1:
+                        value = value + by_corner[a][b // 2][c // 2] * (1.0 / (128 * self.nd))
+                    lots.append(value)
+        tile = jnp.zeros((8, 128), jnp.float32)
+        sub = lax.broadcasted_iota(jnp.int32, (8, 128), 0)
+        for k, value in enumerate(lots):
+            whole = jnp.sum(jnp.sum(value, 0, keepdims=True), -1, keepdims=True)
+            tile = jnp.where((sub == k % 8) & (lane == k // 8), whole, tile)
+        r.tap_part[...] = tile
+
+
+class Refs:
+    def __init__(self, names, refs):
+        for name, ref in zip(names, refs):
+            setattr(self, name, ref)
+
+
+def spectral(measured, point_spread, stencil_weights, upstream):
+    planes, row_count, columns = measured.shape
+    plan = Spectral(lax.axis_size("gy"), lax.axis_size("gz"), planes, row_count, columns)
+    waves = [jnp.asarray(part) for part in wave_rows(columns)]
+    if plan.rows != columns:
+        waves += [jnp.asarray(part) for part in wave_rows(plan.rows)]
+    along = jnp.asarray(axis_values(plan.rows).reshape(9, 1, plan.rows))
+    across = axis_values(columns).reshape(9, 2, plan.nd, plan.bins).transpose(2, 1, 3, 0)
+    frequencies = np.zeros((plan.nd, 2 * plan.bins, 128), np.float32)
+    frequencies[:, :, :9] = across.reshape(plan.nd, 2 * plan.bins, 9)
+    scratch = plan.scratch()
+    inputs = ["weights", "measured", "point_spread", "upstream", "along", "frequencies"]
+    names = inputs + ["wave_%d" % k for k in range(len(waves))] + ["out", "tap_out"] + list(scratch)
+
+    def body(*refs):
+        r = Refs(names, refs)
+        r.tab_x = (r.wave_0, r.wave_1)
+        r.tab_y = (r.wave_2, r.wave_3) if len(waves) > 2 else r.tab_x
+        plan.run(r)
+
+    out, taps = pl.pallas_call(
+        body,
+        out_shape=(
+            jax.ShapeDtypeStruct(measured.shape, jnp.float32),
+            jax.ShapeDtypeStruct((8, 128), jnp.float32),
+        ),
+        in_specs=[SMEM] + [VMEM] * (5 + len(waves)),
+        out_specs=(VMEM, VMEM),
+        scratch_shapes=list(scratch.values()),
+        compiler_params=pltpu.CompilerParams(
+            collective_id=0, has_side_effects=True, vmem_limit_bytes=60 * 1024 * 1024
+        ),
+        name="spectral",
+    )(
+        stencil_weights.reshape(27), measured, point_spread, upstream, along, jnp.asarray(frequencies), *waves
+    )
+    taps = taps[:, :4].T.reshape(32)[:27].reshape(3, 3, 3)
+    return (out, taps)
+
+
 def solution(mesh):
+    def program(measured, point_spread, stencil_weights, upstream):
+        planes, row_count, columns = measured.shape
+        fits = spectral_fits(mesh.shape["gy"], mesh.shape["gz"], planes, row_count, columns)
+        chosen = spectral if fits else local
+        return chosen(measured, point_spread, stencil_weights, upstream)
+
     return jax.shard_map(
-        local,
+        program,
         mesh=mesh,
         in_specs=(P("gz", "gy", None), P("gy", None), P(), P("gz", "gy", None)),
         out_specs=(P("gz", "gy", None), P()),

time: 653 us -> 103 us (0.16); the launches traced: 643 us -> 103 us
  Pallas kernels: 276 us -> 97.8 us
  matrix products: 121 us -> 0 us
  starting transfers between devices: 66.7 us -> 0 us
  local copies, waits for them, and re-layouts: 62.9 us -> 4.7 us
  waiting for transfers between devices: 57.9 us -> 0 us
  other arithmetic: 41.7 us -> 0 us
  between operations: 17 us -> 0.64 us
    pallas_call x8 -> x1, Pallas kernels: 276 us -> 97.8 us  [spectral(): pl.pallas_call(body, out_shape=(jax.ShapeDtypeStruct(measured.shape, jnp....]
    dot_general x28 -> x0, matrix products: 121 us -> none  [contract(): return jnp.einsum(form, left, right, precision=lax.Precision.HIGH)]
    all_to_all x7 -> x0, starting transfers between devices: 66.7 us -> none  [the longest x4 55.3 us: forward(): lax.all_to_all(sent.reshape(groups, row_count, count * 2 * bins), 'gy', s...]
    all_to_all x7 -> x0, waiting for transfers between devices: 57.9 us -> none  [the longest x4 32 us: forward(): lax.all_to_all(sent.reshape(groups, row_count, count * 2 * bins), 'gy', s...]
    reshape x11 -> x3, local copies, waits for them, and re-layouts: 16.3 us -> 2.06 us  [the longest x1 1.29 us: spectral(): stencil_weights.reshape(27)]
    dot_general x8 -> x0, local copies, waits for them, and re-layouts: 11.8 us -> none  [contract(): return jnp.einsum(form, left, right, precision=lax.Precision.HIGH)]
    another operation x5 -> x0, local copies, waits for them, and re-layouts: 11.2 us -> none  [the longest x1 3.74 us: local(): jnp.stack([jnp.sum(residual * residual), jnp.sum(residual * vector_1), jn...]
    cos x2 -> x0, other arithmetic: 9.43 us -> none  [wave_tables(): tables.append(jnp.cos(angle).reshape(half, pair, 2 * bins))]
  transfers between devices with their start and end apart: 7 -> 0, of which waited for: 3 -> 0; matrix products, arithmetic and copies ran while one was open for 13% -> 0% of each run, Pallas kernels for 35% -> 0%
where the time goes in v1:
time: 103 us
  Pallas kernels  97.8 us (95%)
  local copies, waits for them, and re-layouts  4.7 us (5%)
    pallas_call x1, Pallas kernels, spectral(): pl.pallas_call(body, out_shape=(jax.ShapeDtypeStruct(measured.shape, jnp....  97.8 us

profile of v1, /device:TPU:0, one launch (start us, length us, event | category | flops | bytes accessed | tf_op | source)
XLA Modules:
  0.0 103.1 jit_solution(7250048717071669483)
XLA Ops:
  0.6 1.3 %reshape.13.refs_0_ = f32[27]{0:T(128)} reshape(f32[3,3,3]{2,1,0:T(4,128)} %param.10) | data formatting | bytes 216 | tf_op jit(solution)/shard_map/reshape | solution.py:1589
  1.9 97.8 %spectral.1 = (f32[1,128,1024]{2,1,0:T(8,128)}, f32[8,128]{1,0:T(8,128)}) custom-call(f32[27]{0:T(128)} %reshape.13.refs_0_, f32[1,128,1024]{2,1,0:T(8,128)} %refs_1_.1, f32[128,1024]{1,0:T(8,128)} %refs_2_.1, f32[1,128,1024]{2,1,0:T(8,128)} %refs_3_.1, f32[9,1,1024]{2,1,0:T(1,128)} %constant.10.clone.refs_4_, f32[32,32,128]{2,1,0:T(8,128)} %constant.11.clone.refs_5_, ...), custom_call_target="tpu_custom_call" | custom-call | tf_op jit(solution)/shard_map/spectral/pallas_call | solution.py:1575
  99.7 0.7 slice_bitcast_fusion
  100.4 0.1 copy.10
  100.5 0.1 reshape.14
  100.6 0.7 reshape.15
  101.3 1.9 %copy.12 = f32[1,128,1024]{2,1,0:T(8,128)} copy(f32[1,128,1024]{2,1,0:T(8,128)} %get-tuple-element.8) | data formatting | bytes 1048576

commit v2 on v1

--- a/solution.py
+++ b/solution.py
@@ -12,6 +12,7 @@
 SIDES = [(dy, dz) for dy in (-1, 0, 1) for dz in (-1, 0, 1) if (dy, dz) != (0, 0)]
 VMEM = pl.BlockSpec(memory_space=pltpu.VMEM)
 SMEM = pl.BlockSpec(memory_space=pltpu.SMEM)
+HBM = pl.BlockSpec(memory_space=pltpu.HBM)
 
 
 def moved(value, shift):
@@ -492,7 +493,7 @@
     if columns % (16 * devices) or row_count % 128 or rows % 512 or planes != 1 or mesh_z % 2:
         return False
     tiles = 4 * depth // 8 * (rows // 128)
-    return depth < 8 and depth % 2 == 0 and devices % tiles == 0
+    return depth < 8 and depth % 2 == 0 and mesh_y % 4 == 0 and tiles % (2 * mesh_z) == 0
 
 
 def wave_rows(length):
@@ -566,7 +567,7 @@
         self.tiers = self.bins // 8
         self.lanes = self.rows // 128
         self.tiles = 4 * self.depth // 8 * self.lanes
-        self.stride = self.nd // self.tiles
+        self.share = self.tiles // (2 * self.nz)
 
     def place_of(self, index):
         return (lax.rem(index, self.ny), lax.div(index, self.ny))
@@ -618,24 +619,23 @@
             cols_mw=pltpu.VMEM((2, 8, self.rows), F),
             edge_cols=pltpu.VMEM((2, 8, self.rows), F),
             part=pltpu.VMEM((3, 3, self.tiles, 8, 128), F),
-            slots=pltpu.VMEM((3, 3, nd, 8, 128), F),
-            sums=pltpu.VMEM((3, 3, 8, 128), F),
+            slots=pltpu.VMEM((3, 3, nd, self.share, 8, 128), F),
+            sums=pltpu.VMEM((3, 3, self.share, 8, 128), F),
             full=pltpu.VMEM((3, 3, self.tiles, 8, 128), F),
             acc=pltpu.VMEM((8, 8, 128), F),
-            total=pltpu.VMEM((2, 8, 8, 128), F),
             taps=pltpu.VMEM((27, 8, 128), F),
-            tap_part=pltpu.VMEM((8, 128), F),
-            tap_slots=pltpu.VMEM((nd, 8, 128), F),
+            tap_part=pltpu.VMEM((1, 128), F),
+            tap_slots=pltpu.VMEM((nd, 1, 128), F),
             sent_o=pltpu.VMEM(packed, F),
             got_o=pltpu.VMEM((nd, 2, bins, self.row_count), F),
             send_big=D((2, nd)),
             recv_big=D((2, nd)),
             send_p=D((self.ny,)),
             recv_p=D((self.ny,)),
-            send_part=D((2, 3, self.tiles)),
+            send_part=D((2, 3, 2 * self.nz)),
             recv_part=D((2, 3, nd)),
             send_full=D((2, 3, nd)),
-            recv_full=D((2, 3, self.tiles)),
+            recv_full=D((2, 3, 2 * self.nz)),
             send_tap=D((nd,)),
             recv_tap=D((nd,)),
         )
@@ -655,12 +655,18 @@
             sent.at[peer], got.at[z, :, :, lanes], r.send_big.at[lot, peer], r.recv_big.at[lot, source], peer
         )
 
-    def spread_start(self, r, sent, got, lot):
-        @pl.loop(1, self.nd)
+    def spread_start(self, r, sent, got, lot, quarter=None):
+        first, end = (1, self.nd)
+        if quarter is not None:
+            first, end = (max(1, quarter * self.nd // 4), (quarter + 1) * self.nd // 4)
+
+        @pl.loop(first, end)
         def _(k):
             peer = lax.rem(self.me + k, self.nd)
             self.spread_copy(r, sent, got, lot, peer, self.me).start()
 
+        if quarter:
+            return
         y, z = self.place_of(self.me)
         lanes = pl.ds(pl.multiple_of(y * self.row_count, 128), self.row_count)
         got[z, :, :, lanes] = sent[self.me]
@@ -710,101 +716,94 @@
             r.sent_o.at[z, :, :, lanes], r.got_o.at[source], r.send_big.at[0, peer], r.recv_big.at[0, source], peer
         )
 
-    def owner(self, kind, tile):
-        if kind == 0:
-            return tile * self.stride
-        if kind == 1:
-            return tile * self.stride + self.stride - 1
-        return self.nd - 1
+    def owner(self, kind, number):
+        if kind == 2:
+            number = self.nz
+        return lax.rem(number, self.nz) * self.ny + self.ny // 2 - 1 + 2 * lax.div(number, self.nz)
 
     def owned(self, kind):
-        if kind == 0:
-            return lax.rem(self.me, self.stride) == 0
-        if kind == 1:
-            return lax.rem(self.me, self.stride) == self.stride - 1
-        return self.me == self.nd - 1
-
-    def counts(self, kind):
-        return 1 if kind == 2 else self.tiles
+        low = self.ny // 2 - 1
+        if kind == 2:
+            return self.me == self.owner(2, 0)
+        return (self.y == low) | (self.y == low + 2)
+
+    def owners(self, kind):
+        return 1 if kind == 2 else 2 * self.nz
 
     def mine(self, kind):
-        return 0 if kind == 2 else lax.div(self.me, self.stride)
+        return 0 if kind == 2 else jnp.where(self.y == self.ny // 2 - 1, 0, self.nz) + self.z
+
+    def lot(self, ref, turn, kind, number):
+        count = 1 if kind == 2 else self.share
+        return ref.at[turn, kind, pl.ds(number * count, count)]
+
+    def slot(self, r, turn, kind, source):
+        return r.slots.at[turn, kind, source, pl.ds(0, 1 if kind == 2 else self.share)]
+
+    def part_copy(self, r, turn, kind, number, source, peer):
+        return self.remote(
+            self.lot(r.part, turn, kind, number), self.slot(r, turn, kind, source),
+            r.send_part.at[turn % 2, kind, number], r.recv_part.at[turn % 2, kind, source], peer,
+        )
+
+    def full_copy(self, r, turn, kind, number, peer):
+        return self.remote(
+            r.sums.at[turn, kind, pl.ds(0, 1 if kind == 2 else self.share)], self.lot(r.full, turn, kind, number),
+            r.send_full.at[turn % 2, kind, peer], r.recv_full.at[turn % 2, kind, number], peer,
+        )
 
     def reduce_start(self, r, turn, kinds):
-        lot = turn % 2
         for kind in kinds:
 
-            @pl.loop(0, self.counts(kind))
-            def _(tile):
-                owner = self.owner(kind, tile)
+            @pl.loop(0, self.owners(kind))
+            def _(number):
+                owner = self.owner(kind, number)
 
                 @pl.when(owner != self.me)
                 def _():
-                    self.remote(
-                        r.part.at[turn, kind, tile], r.slots.at[turn, kind, self.me],
-                        r.send_part.at[lot, kind, tile], r.recv_part.at[lot, kind, self.me], owner,
-                    ).start()
-
-    def reduce_finish(self, r, turn, kinds):
-        lot = turn % 2
+                    self.part_copy(r, turn, kind, number, self.me, owner).start()
+
+    def reduce_middle(self, r, turn, kinds):
         for kind in kinds:
 
             @pl.when(self.owned(kind))
             def _():
-                tile = self.mine(kind)
-                r.slots[turn, kind, self.me] = r.part[turn, kind, tile]
+                number = self.mine(kind)
+                self.slot(r, turn, kind, self.me)[...] = self.lot(r.part, turn, kind, number)[...]
 
                 @pl.loop(1, self.nd)
                 def _(k):
                     peer = lax.rem(self.me + k, self.nd)
-                    self.remote(
-                        r.part.at[turn, kind, tile], r.slots.at[turn, kind, peer],
-                        r.send_part.at[lot, kind, tile], r.recv_part.at[lot, kind, peer], peer,
-                    ).wait_recv()
-
-                lots = [r.slots[turn, kind, k] for k in range(self.nd)]
+                    self.part_copy(r, turn, kind, number, peer, peer).wait_recv()
+
+                lots = [self.slot(r, turn, kind, k)[...] for k in range(self.nd)]
                 while len(lots) > 1:
                     lots = [lots[k] + lots[k + 1] for k in range(0, len(lots) - 1, 2)] + lots[len(lots) // 2 * 2 :]
-                r.sums[turn, kind] = lots[0]
+                r.sums[turn, kind, pl.ds(0, 1 if kind == 2 else self.share)] = lots[0]
 
                 @pl.loop(1, self.nd)
                 def _(k):
-                    peer = lax.rem(self.me + k, self.nd)
-                    self.remote(
-                        r.sums.at[turn, kind], r.full.at[turn, kind, tile],
-                        r.send_full.at[lot, kind, peer], r.recv_full.at[lot, kind, tile], peer,
-                    ).start()
-
-                r.full[turn, kind, tile] = r.sums[turn, kind]
-
+                    self.full_copy(r, turn, kind, number, lax.rem(self.me + k, self.nd)).start()
+
+                self.lot(r.full, turn, kind, number)[...] = lots[0]
+
+    def reduce_end(self, r, turn, kinds):
         for kind in kinds:
 
-            @pl.loop(0, self.counts(kind))
-            def _(tile):
-                owner = self.owner(kind, tile)
+            @pl.loop(0, self.owners(kind))
+            def _(number):
+                owner = self.owner(kind, number)
 
                 @pl.when(owner != self.me)
                 def _():
-                    self.remote(
-                        r.sums.at[turn, kind], r.full.at[turn, kind, tile],
-                        r.send_full.at[lot, kind, owner], r.recv_full.at[lot, kind, tile], owner,
-                    ).wait_recv()
-                    self.remote(
-                        r.part.at[turn, kind, tile], r.slots.at[turn, kind, self.me],
-                        r.send_part.at[lot, kind, tile], r.recv_part.at[lot, kind, self.me], owner,
-                    ).wait_send()
+                    self.full_copy(r, turn, kind, number, owner).wait_recv()
+                    self.part_copy(r, turn, kind, number, self.me, owner).wait_send()
 
             @pl.when(self.owned(kind))
             def _():
-                tile = self.mine(kind)
-
                 @pl.loop(1, self.nd)
                 def _(k):
-                    peer = lax.rem(self.me + k, self.nd)
-                    self.remote(
-                        r.sums.at[turn, kind], r.full.at[turn, kind, tile],
-                        r.send_full.at[lot, kind, peer], r.recv_full.at[lot, kind, tile], peer,
-                    ).wait_send()
+                    self.full_copy(r, turn, kind, self.mine(kind), lax.rem(self.me + k, self.nd)).wait_send()
 
 
     def row_spectra(self, r, source, sent):
@@ -1213,7 +1212,7 @@
         self.me = self.z * self.ny + self.y
 
         def w(a, b, c):
-            return r.weights[9 * a + 3 * b + c]
+            return r.weights[a, b, c]
 
         barrier = pltpu.get_barrier_semaphore()
 
@@ -1223,26 +1222,42 @@
                 barrier, inc=1, device_id=self.place_of(lax.rem(self.me + k, self.nd)), device_id_type=MESH
             )
 
-        own = r.frequencies[self.me]
+        def load(name):
+            far = getattr(r, "far_" + name)
+            far = far.at[self.me] if name == "frequencies" else far
+            return pltpu.make_async_copy(far, getattr(r, name), r.loaded.at[r.inputs.index(name)])
+
+        tables = [name for name in r.inputs if name.startswith("wave")]
+        order = ["frequencies", "weights", "along", "point_spread"] + tables + ["measured", "upstream"]
+        for name in order:
+            load(name).start()
+        load("frequencies").wait()
         for which in range(9):
             for part in range(2):
                 r.across[which, part] = jnp.broadcast_to(
-                    own[part * self.bins : (part + 1) * self.bins, which : which + 1], (self.bins, 128)
+                    r.frequencies[part * self.bins : (part + 1) * self.bins, which : which + 1], (self.bins, 128)
                 )
+        load("along").wait()
+        load("weights").wait()
+        self.build_stencil(r, w)
+        load("point_spread").wait()
+        for name in tables:
+            load(name).wait()
         self.point_spectra(r, r.point_spread[...])
+        load("measured").wait()
         self.row_spectra(r, r.measured[0], r.sent_m)
         pl.semaphore_wait(barrier, self.nd - 1)
         self.point_start(r)
         self.spread_start(r, r.sent_m, r.got_m, 0)
+        load("upstream").wait()
         self.row_spectra(r, r.upstream[0], r.sent_u)
-        self.spread_start(r, r.sent_u, r.got_u, 1)
-        self.build_stencil(r, w)
         self.clear(r.rows_v0, r.rows_v1, r.rows_v2, r.rows_up, r.acc, r.taps)
 
         self.point_wait(r)
         self.column_spectra(r, r.got_p, r.wave_p)
         self.build_blur(r)
         self.spread_wait(r, r.sent_m, r.got_m, 0)
+        self.spread_start(r, r.sent_u, r.got_u, 1, 0)
         self.column_spectra(r, r.got_m, r.wave)
 
         def start(tier, step, masks, columns):
@@ -1256,8 +1271,11 @@
 
         self.sweep(start)
         self.reduce_start(r, 0, [0])
+        self.spread_start(r, r.sent_u, r.got_u, 1, 1)
         self.settle(r.rows_v0)
-        self.reduce_finish(r, 0, [0])
+        self.reduce_middle(r, 0, [0])
+        self.reduce_end(r, 0, [0])
+        self.spread_start(r, r.sent_u, r.got_u, 1, 2)
         self.unpack(r.full.at[0, 0], r.cols_v0)
 
         def first(tier, step, masks, columns, back):
@@ -1274,7 +1292,9 @@
         self.stencil_twice(r, w, r.v0, r.rows_v0, r.cols_v0, r.m0, r.rows_m0, r.cols_m0, first)
         self.scalars_out(r, 1, 3)
         self.reduce_start(r, 1, [0, 2])
+        self.spread_start(r, r.sent_u, r.got_u, 1, 3)
         self.settle(r.rows_v1)
+        self.reduce_middle(r, 1, [0, 2])
         self.spread_wait(r, r.sent_u, r.got_u, 1)
         self.column_spectra(r, r.got_u, r.wave)
 
@@ -1288,7 +1308,7 @@
         self.sweep(upper)
         self.settle(r.rows_up)
         self.clear(r.acc)
-        self.reduce_finish(r, 1, [0, 2])
+        self.reduce_end(r, 1, [0, 2])
         self.reduce_start(r, 2, [1])
         self.unpack(r.full.at[1, 0], r.cols_v1)
         norm_0, curve_0, image_0 = self.scalars_in(r, 1, 3)
@@ -1313,7 +1333,8 @@
         self.scalars_out(r, 2, 7)
         self.reduce_start(r, 2, [0, 2])
         self.settle(r.rows_v2)
-        self.reduce_finish(r, 2, [0, 1, 2])
+        self.reduce_middle(r, 2, [1, 0, 2])
+        self.reduce_end(r, 2, [1, 0, 2])
         self.unpack(r.full.at[2, 0], r.cols_v2)
         self.unpack(r.full.at[2, 1], r.cols_up)
 
@@ -1420,7 +1441,12 @@
         lots = [r.tap_slots[k] for k in range(self.nd)]
         while len(lots) > 1:
             lots = [lots[k] + lots[k + 1] for k in range(0, len(lots) - 1, 2)] + lots[len(lots) // 2 * 2 :]
-        r.tap_out[...] = lots[0] / math.sqrt(self.depth * self.rows * self.columns)
+        line = jnp.broadcast_to(lots[0] / math.sqrt(self.depth * self.rows * self.columns), (8, 128))
+        for a in range(3):
+            for b in range(3):
+                first = 9 * a + 3 * b
+                turned = pltpu.roll(line, 128 - first, 1) if first else line
+                r.tap_out[a, pl.ds(b, 1)] = turned[:1, :3]
 
     def tap_sums(self, r, weight):
         Z = self.depth
@@ -1513,7 +1539,6 @@
                         term = extra * self.shifted(at_x[1 - edge], a - 1) * at_m[edge]
                         by_corner[a][edge][k] = by_corner[a][edge][k] + term
 
-        lane = lax.broadcasted_iota(jnp.int32, (8, 128), 1)
         lots = []
         for a in range(3):
             s = [r.taps[9 * a + k] for k in range(9)]
@@ -1538,12 +1563,12 @@
                     if b != 1 and c != 1:
                         value = value + by_corner[a][b // 2][c // 2] * (1.0 / (128 * self.nd))
                     lots.append(value)
-        tile = jnp.zeros((8, 128), jnp.float32)
-        sub = lax.broadcasted_iota(jnp.int32, (8, 128), 0)
+        lane = lax.broadcasted_iota(jnp.int32, (1, 128), 1)
+        line = jnp.zeros((1, 128), jnp.float32)
         for k, value in enumerate(lots):
             whole = jnp.sum(jnp.sum(value, 0, keepdims=True), -1, keepdims=True)
-            tile = jnp.where((sub == k % 8) & (lane == k // 8), whole, tile)
-        r.tap_part[...] = tile
+            line = jnp.where(lane == k, whole, line)
+        r.tap_part[...] = line
 
 
 class Refs:
@@ -1563,32 +1588,39 @@
     frequencies = np.zeros((plan.nd, 2 * plan.bins, 128), np.float32)
     frequencies[:, :, :9] = across.reshape(plan.nd, 2 * plan.bins, 9)
     scratch = plan.scratch()
-    inputs = ["weights", "measured", "point_spread", "upstream", "along", "frequencies"]
-    names = inputs + ["wave_%d" % k for k in range(len(waves))] + ["out", "tap_out"] + list(scratch)
+    arrays = dict(weights=stencil_weights, measured=measured, point_spread=point_spread, upstream=upstream, along=along)
+    arrays.update({"wave_%d" % k: part for k, part in enumerate(waves)})
+    arrays["frequencies"] = jnp.asarray(frequencies)
+    for name, array in arrays.items():
+        shape = array.shape[1:] if name == "frequencies" else array.shape
+        space = pltpu.SMEM if name == "weights" else pltpu.VMEM
+        scratch[name] = space(shape, array.dtype)
+    scratch["loaded"] = pltpu.SemaphoreType.DMA((len(arrays),))
+    names = ["far_" + name for name in arrays] + ["out", "tap_out"] + list(scratch)
 
     def body(*refs):
         r = Refs(names, refs)
         r.tab_x = (r.wave_0, r.wave_1)
         r.tab_y = (r.wave_2, r.wave_3) if len(waves) > 2 else r.tab_x
+        r.inputs = list(arrays)
         plan.run(r)
 
     out, taps = pl.pallas_call(
         body,
         out_shape=(
             jax.ShapeDtypeStruct(measured.shape, jnp.float32),
-            jax.ShapeDtypeStruct((8, 128), jnp.float32),
+            jax.ShapeDtypeStruct((3, 3, 3), jnp.float32),
         ),
-        in_specs=[SMEM] + [VMEM] * (5 + len(waves)),
+        in_specs=[HBM] * len(arrays),
         out_specs=(VMEM, VMEM),
         scratch_shapes=list(scratch.values()),
         compiler_params=pltpu.CompilerParams(
-            collective_id=0, has_side_effects=True, vmem_limit_bytes=60 * 1024 * 1024
+            collective_id=0, has_side_effects=True, vmem_limit_bytes=32 * 1024 * 1024
         ),
         name="spectral",
     )(
-        stencil_weights.reshape(27), measured, point_spread, upstream, along, jnp.asarray(frequencies), *waves
+        *(pltpu.with_memory_space_constraint(array, pltpu.HBM) for array in arrays.values())
     )
-    taps = taps[:, :4].T.reshape(32)[:27].reshape(3, 3, 3)
     return (out, taps)
 
 

time: 103 us -> 85 us (0.83)
  Pallas kernels: 97.8 us -> 82.7 us
  local copies, waits for them, and re-layouts: 4.7 us -> 1.39 us
    pallas_call x1, Pallas kernels: 97.8 us -> 82.7 us  [spectral(): pl.pallas_call(body, out_shape=(jax.ShapeDtypeStruct(measured.shape, jnp....]
    reshape x3 -> x0, local copies, waits for them, and re-layouts: 2.06 us -> none  [the longest x1 1.29 us: spectral(): stencil_weights.reshape(27)]
where the time goes in v2:
time: 85 us; the launch traced here: 84.8 us
  Pallas kernels  82.7 us (97%)
  local copies, waits for them, and re-layouts  1.39 us (2%)
    pallas_call x1, Pallas kernels, spectral(): pl.pallas_call(body, out_shape=(jax.ShapeDtypeStruct(measured.shape, jnp....  82.7 us

profile of v2, /device:TPU:0, one launch (start us, length us, event | category | flops | bytes accessed | tf_op | source)
XLA Modules:
  0.0 84.8 jit_solution(331427586645604871)
XLA Ops:
  0.6 82.7 %spectral.1 = (f32[1,128,1024]{2,1,0:T(8,128)S(1)}, f32[3,3,3]{2,1,0:T(4,128)S(1)}) custom-call(f32[3,3,3]{2,1,0:T(4,128)} %refs_0_.1, f32[1,128,1024]{2,1,0:T(8,128)} %refs_1_.1, f32[128,1024]{1,0:T(8,128)} %refs_2_.1, f32[1,128,1024]{2,1,0:T(8,128)} %refs_3_.1, f32[9,1,1024]{2,1,0:T(1,128)} %constant.10.clone.refs_4_, ...), custom_call_target="tpu_custom_call" | custom-call | tf_op jit(solution)/shard_map/spectral/pallas_call | solution.py:1608
  83.4 0.8 copy.12
  84.2 0.6 copy.13

commit v3 on v2

--- a/solution.py
+++ b/solution.py
@@ -579,6 +579,7 @@
         edge = (2, Z, 2, bins, 128)
         F = jnp.float32
         D = pltpu.SemaphoreType.DMA
+        others = nd - 1
         names = dict(
             sent_m=pltpu.VMEM((nd, 2, bins, 128 * (self.row_count // 128)), F),
             sent_u=pltpu.VMEM((nd, 2, bins, self.row_count), F),
@@ -619,7 +620,7 @@
             cols_mw=pltpu.VMEM((2, 8, self.rows), F),
             edge_cols=pltpu.VMEM((2, 8, self.rows), F),
             part=pltpu.VMEM((3, 3, self.tiles, 8, 128), F),
-            slots=pltpu.VMEM((3, 3, nd, self.share, 8, 128), F),
+            slots=pltpu.VMEM((3, 3, others, self.share, 8, 128), F),
             sums=pltpu.VMEM((3, 3, self.share, 8, 128), F),
             full=pltpu.VMEM((3, 3, self.tiles, 8, 128), F),
             acc=pltpu.VMEM((8, 8, 128), F),
@@ -628,16 +629,16 @@
             tap_slots=pltpu.VMEM((nd, 1, 128), F),
             sent_o=pltpu.VMEM(packed, F),
             got_o=pltpu.VMEM((nd, 2, bins, self.row_count), F),
-            send_big=D((2, nd)),
-            recv_big=D((2, nd)),
-            send_p=D((self.ny,)),
-            recv_p=D((self.ny,)),
-            send_part=D((2, 3, 2 * self.nz)),
-            recv_part=D((2, 3, nd)),
-            send_full=D((2, 3, nd)),
-            recv_full=D((2, 3, 2 * self.nz)),
-            send_tap=D((nd,)),
-            recv_tap=D((nd,)),
+            send_big=D((3,)),
+            recv_big=D((3,)),
+            send_p=D,
+            recv_p=D,
+            send_part=D((2, 3)),
+            recv_part=D((2, 3)),
+            send_full=D((2, 3)),
+            recv_full=D((2, 3)),
+            send_tap=D,
+            recv_tap=D,
         )
         return names
 
@@ -648,73 +649,56 @@
             device_id=self.place_of(peer), device_id_type=MESH,
         )
 
-    def spread_copy(self, r, sent, got, lot, peer, source):
-        y, z = self.place_of(source)
-        lanes = pl.ds(pl.multiple_of(y * self.row_count, 128), self.row_count)
-        return self.remote(
-            sent.at[peer], got.at[z, :, :, lanes], r.send_big.at[lot, peer], r.recv_big.at[lot, source], peer
-        )
+    def arrived(self, shape, semaphore):
+        self.remote(shape, shape, semaphore, semaphore, self.me).wait_recv()
+
+    def row_lanes(self, y):
+        return pl.ds(pl.multiple_of(y * self.row_count, 128), self.row_count)
 
     def spread_start(self, r, sent, got, lot, quarter=None):
         first, end = (1, self.nd)
         if quarter is not None:
             first, end = (max(1, quarter * self.nd // 4), (quarter + 1) * self.nd // 4)
+        here = got.at[self.z, :, :, self.row_lanes(self.y)]
 
         @pl.loop(first, end)
         def _(k):
             peer = lax.rem(self.me + k, self.nd)
-            self.spread_copy(r, sent, got, lot, peer, self.me).start()
-
-        if quarter:
-            return
-        y, z = self.place_of(self.me)
-        lanes = pl.ds(pl.multiple_of(y * self.row_count, 128), self.row_count)
-        got[z, :, :, lanes] = sent[self.me]
-
-    def spread_wait(self, r, sent, got, lot):
+            self.remote(sent.at[peer], here, r.send_big.at[lot], r.recv_big.at[lot], peer).start()
+
+        if not quarter:
+            here[...] = sent[self.me]
+
+    def spread_wait(self, r, sent, lot):
+        others = sent.at[pl.ds(0, self.nd - 1)]
+        self.arrived(others, r.recv_big.at[lot])
+        self.arrived(others, r.send_big.at[lot])
+
+    def point_start(self, r):
+        here = r.got_p.at[:, :, self.row_lanes(self.y)]
+
+        @pl.loop(1, self.ny)
+        def _(k):
+            peer = lax.rem(self.y + k, self.ny)
+            self.remote(r.sent_p.at[peer], here, r.send_p, r.recv_p, self.z * self.ny + peer).start()
+
+        here[...] = r.sent_p[self.y]
+
+    def point_wait(self, r):
+        others = r.sent_p.at[pl.ds(0, self.ny - 1)]
+        self.arrived(others, r.recv_p)
+        self.arrived(others, r.send_p)
+
+    def return_start(self, r):
         @pl.loop(1, self.nd)
         def _(k):
             peer = lax.rem(self.me + k, self.nd)
-            copy = self.spread_copy(r, sent, got, lot, peer, peer)
-            copy.wait_recv()
-
-        @pl.loop(1, self.nd)
-        def _(k):
-            peer = lax.rem(self.me + k, self.nd)
-            self.spread_copy(r, sent, got, lot, peer, self.me).wait_send()
-
-    def point_copy(self, r, peer_y, source_y):
-        lanes = pl.ds(pl.multiple_of(source_y * self.row_count, 128), self.row_count)
-        return self.remote(
-            r.sent_p.at[peer_y], r.got_p.at[:, :, lanes], r.send_p.at[peer_y], r.recv_p.at[source_y],
-            self.z * self.ny + peer_y,
-        )
-
-    def point_start(self, r):
-        @pl.loop(1, self.ny)
-        def _(k):
-            self.point_copy(r, lax.rem(self.y + k, self.ny), self.y).start()
-
-        lanes = pl.ds(pl.multiple_of(self.y * self.row_count, 128), self.row_count)
-        r.got_p[:, :, lanes] = r.sent_p[self.y]
-
-    def point_wait(self, r):
-        @pl.loop(1, self.ny)
-        def _(k):
-            peer = lax.rem(self.y + k, self.ny)
-            self.point_copy(r, peer, peer).wait_recv()
-
-        @pl.loop(1, self.ny)
-        def _(k):
-            peer = lax.rem(self.y + k, self.ny)
-            self.point_copy(r, peer, self.y).wait_send()
-
-    def return_copy(self, r, peer, source):
-        y, z = self.place_of(peer)
-        lanes = pl.ds(pl.multiple_of(y * self.row_count, 128), self.row_count)
-        return self.remote(
-            r.sent_o.at[z, :, :, lanes], r.got_o.at[source], r.send_big.at[0, peer], r.recv_big.at[0, source], peer
-        )
+            y, z = self.place_of(peer)
+            self.remote(
+                r.sent_o.at[z, :, :, self.row_lanes(y)], r.got_o.at[self.me], r.send_big.at[2], r.recv_big.at[2], peer
+            ).start()
+
+        r.got_o[self.me] = r.sent_o[self.z, :, :, self.row_lanes(self.y)]
 
     def owner(self, kind, number):
         if kind == 2:
@@ -733,27 +717,19 @@
     def mine(self, kind):
         return 0 if kind == 2 else jnp.where(self.y == self.ny // 2 - 1, 0, self.nz) + self.z
 
-    def lot(self, ref, turn, kind, number):
-        count = 1 if kind == 2 else self.share
-        return ref.at[turn, kind, pl.ds(number * count, count)]
-
-    def slot(self, r, turn, kind, source):
-        return r.slots.at[turn, kind, source, pl.ds(0, 1 if kind == 2 else self.share)]
-
-    def part_copy(self, r, turn, kind, number, source, peer):
-        return self.remote(
-            self.lot(r.part, turn, kind, number), self.slot(r, turn, kind, source),
-            r.send_part.at[turn % 2, kind, number], r.recv_part.at[turn % 2, kind, source], peer,
-        )
-
-    def full_copy(self, r, turn, kind, number, peer):
-        return self.remote(
-            r.sums.at[turn, kind, pl.ds(0, 1 if kind == 2 else self.share)], self.lot(r.full, turn, kind, number),
-            r.send_full.at[turn % 2, kind, peer], r.recv_full.at[turn % 2, kind, number], peer,
-        )
+    def width(self, kind):
+        return 1 if kind == 2 else self.share
+
+    def lot(self, ref, turn, kind, number, count=1):
+        count = count * self.width(kind)
+        return ref.at[turn, kind, pl.ds(number * self.width(kind), count)]
+
+    def slot(self, r, turn, kind, first, count=1):
+        return r.slots.at[turn, kind, pl.ds(first, count), pl.ds(0, self.width(kind))]
 
     def reduce_start(self, r, turn, kinds):
         for kind in kinds:
+            send, receive = (r.send_part.at[turn % 2, kind], r.recv_part.at[turn % 2, kind])
 
             @pl.loop(0, self.owners(kind))
             def _(number):
@@ -761,49 +737,52 @@
 
                 @pl.when(owner != self.me)
                 def _():
-                    self.part_copy(r, turn, kind, number, self.me, owner).start()
+                    place = lax.rem(self.me - owner + self.nd, self.nd) - 1
+                    self.remote(
+                        self.lot(r.part, turn, kind, number), self.slot(r, turn, kind, place).at[0], send, receive, owner
+                    ).start()
 
     def reduce_middle(self, r, turn, kinds):
+        others = self.nd - 1
         for kind in kinds:
+            send, receive = (r.send_full.at[turn % 2, kind], r.recv_full.at[turn % 2, kind])
 
             @pl.when(self.owned(kind))
             def _():
                 number = self.mine(kind)
-                self.slot(r, turn, kind, self.me)[...] = self.lot(r.part, turn, kind, number)[...]
+                self.arrived(self.slot(r, turn, kind, 0, others), r.recv_part.at[turn % 2, kind])
+                lots = [self.lot(r.part, turn, kind, number)[...]]
+                lots += [self.slot(r, turn, kind, k)[0] for k in range(others)]
+                while len(lots) > 1:
+                    lots = [lots[k] + lots[k + 1] for k in range(0, len(lots) - 1, 2)] + lots[len(lots) // 2 * 2 :]
+                sums = r.sums.at[turn, kind, pl.ds(0, self.width(kind))]
+                sums[...] = lots[0]
 
                 @pl.loop(1, self.nd)
                 def _(k):
-                    peer = lax.rem(self.me + k, self.nd)
-                    self.part_copy(r, turn, kind, number, peer, peer).wait_recv()
-
-                lots = [self.slot(r, turn, kind, k)[...] for k in range(self.nd)]
-                while len(lots) > 1:
-                    lots = [lots[k] + lots[k + 1] for k in range(0, len(lots) - 1, 2)] + lots[len(lots) // 2 * 2 :]
-                r.sums[turn, kind, pl.ds(0, 1 if kind == 2 else self.share)] = lots[0]
-
-                @pl.loop(1, self.nd)
-                def _(k):
-                    self.full_copy(r, turn, kind, number, lax.rem(self.me + k, self.nd)).start()
+                    self.remote(
+                        sums, self.lot(r.full, turn, kind, number), send, receive, lax.rem(self.me + k, self.nd)
+                    ).start()
 
                 self.lot(r.full, turn, kind, number)[...] = lots[0]
 
     def reduce_end(self, r, turn, kinds):
         for kind in kinds:
-
-            @pl.loop(0, self.owners(kind))
-            def _(number):
-                owner = self.owner(kind, number)
-
-                @pl.when(owner != self.me)
-                def _():
-                    self.full_copy(r, turn, kind, number, owner).wait_recv()
-                    self.part_copy(r, turn, kind, number, self.me, owner).wait_send()
+            count = self.owners(kind)
+
+            def finish(count):
+                if count:
+                    self.arrived(self.lot(r.full, turn, kind, 0, count), r.recv_full.at[turn % 2, kind])
+                    self.arrived(self.lot(r.part, turn, kind, 0, count), r.send_part.at[turn % 2, kind])
 
             @pl.when(self.owned(kind))
             def _():
-                @pl.loop(1, self.nd)
-                def _(k):
-                    self.full_copy(r, turn, kind, self.mine(kind), lax.rem(self.me + k, self.nd)).wait_send()
+                finish(count - 1)
+                self.arrived(self.slot(r, turn, kind, 0, self.nd - 1), r.send_full.at[turn % 2, kind])
+
+            @pl.when(jnp.logical_not(self.owned(kind)))
+            def _():
+                finish(count)
 
 
     def row_spectra(self, r, source, sent):
@@ -1256,7 +1235,7 @@
         self.point_wait(r)
         self.column_spectra(r, r.got_p, r.wave_p)
         self.build_blur(r)
-        self.spread_wait(r, r.sent_m, r.got_m, 0)
+        self.spread_wait(r, r.sent_m, 0)
         self.spread_start(r, r.sent_u, r.got_u, 1, 0)
         self.column_spectra(r, r.got_m, r.wave)
 
@@ -1295,7 +1274,7 @@
         self.spread_start(r, r.sent_u, r.got_u, 1, 3)
         self.settle(r.rows_v1)
         self.reduce_middle(r, 1, [0, 2])
-        self.spread_wait(r, r.sent_u, r.got_u, 1)
+        self.spread_wait(r, r.sent_u, 1)
         self.column_spectra(r, r.got_u, r.wave)
 
         def upper(tier, step, masks, columns):
@@ -1405,39 +1384,21 @@
         self.stencil_twice(r, w, r.w3, r.rows_w3, r.cols_w3, r.mw, r.rows_mw, r.cols_mw, last)
         self.column_values(r, r.wave, r.sent_o)
 
-        @pl.loop(1, self.nd)
-        def _(k):
-            self.return_copy(r, lax.rem(self.me + k, self.nd), self.me).start()
-
-        lanes = pl.ds(pl.multiple_of(self.y * self.row_count, 128), self.row_count)
-        r.got_o[self.me] = r.sent_o[self.z, :, :, lanes]
-
+        self.return_start(r)
         self.tap_sums(r, 2.0 * g3)
 
         @pl.loop(1, self.nd)
         def _(k):
             peer = lax.rem(self.me + k, self.nd)
-            self.remote(
-                r.tap_part, r.tap_slots.at[self.me], r.send_tap.at[peer], r.recv_tap.at[self.me], peer
-            ).start()
+            self.remote(r.tap_part, r.tap_slots.at[self.me], r.send_tap, r.recv_tap, peer).start()
 
         r.tap_slots[self.me] = r.tap_part[...]
-
-        @pl.loop(1, self.nd)
-        def _(k):
-            peer = lax.rem(self.me + k, self.nd)
-            self.return_copy(r, peer, peer).wait_recv()
-
+        others = pl.ds(0, self.nd - 1)
+        self.arrived(r.got_o.at[others], r.recv_big.at[2])
         self.row_values(r, r.got_o, r.out)
-
-        @pl.loop(1, self.nd)
-        def _(k):
-            peer = lax.rem(self.me + k, self.nd)
-            self.return_copy(r, peer, self.me).wait_send()
-            self.remote(
-                r.tap_part, r.tap_slots.at[peer], r.send_tap.at[peer], r.recv_tap.at[peer], peer
-            ).wait()
-
+        self.arrived(r.got_o.at[others], r.send_big.at[2])
+        self.arrived(r.tap_slots.at[others], r.recv_tap)
+        self.arrived(r.tap_slots.at[others], r.send_tap)
         lots = [r.tap_slots[k] for k in range(self.nd)]
         while len(lots) > 1:
             lots = [lots[k] + lots[k + 1] for k in range(0, len(lots) - 1, 2)] + lots[len(lots) // 2 * 2 :]

time: 85 us -> 77.9 us (0.916)
  Pallas kernels: 82.7 us -> 75.6 us
    pallas_call x1, Pallas kernels: 82.7 us -> 75.6 us  [spectral(): pl.pallas_call(body, out_shape=(jax.ShapeDtypeStruct(measured.shape, jnp....]
where the time goes in v3:
time: 77.9 us; the launch traced here: 77.6 us
  Pallas kernels  75.6 us (97%)
  local copies, waits for them, and re-layouts  1.39 us (2%)
    pallas_call x1, Pallas kernels, spectral(): pl.pallas_call(body, out_shape=(jax.ShapeDtypeStruct(measured.shape, jnp....  75.6 us

profile of v3, /device:TPU:0, one launch (start us, length us, event | category | flops | bytes accessed | tf_op | source)
XLA Modules:
  0.0 77.6 jit_solution(7256612532573255551)
XLA Ops:
  0.6 75.6 %spectral.1 = (f32[1,128,1024]{2,1,0:T(8,128)S(1)}, f32[3,3,3]{2,1,0:T(4,128)S(1)}) custom-call(f32[3,3,3]{2,1,0:T(4,128)} %refs_0_.1, f32[1,128,1024]{2,1,0:T(8,128)} %refs_1_.1, f32[128,1024]{1,0:T(8,128)} %refs_2_.1, f32[1,128,1024]{2,1,0:T(8,128)} %refs_3_.1, f32[9,1,1024]{2,1,0:T(1,128)} %constant.10.clone.refs_4_, ...), custom_call_target="tpu_custom_call" | custom-call | tf_op jit(solution)/shard_map/spectral/pallas_call | solution.py:1569
  76.3 0.8 %copy.12 = f32[1,128,1024]{2,1,0:T(8,128)} copy(f32[1,128,1024]{2,1,0:T(8,128)S(1)} %get-tuple-element.4) | data formatting | bytes 1048576
  77.1 0.6 copy.13

commit v4 on v3

--- a/solution.py
+++ b/solution.py
@@ -492,8 +492,8 @@
     devices, rows, depth = (mesh_y * mesh_z, row_count * mesh_y, planes * mesh_z)
     if columns % (16 * devices) or row_count % 128 or rows % 512 or planes != 1 or mesh_z % 2:
         return False
-    tiles = 4 * depth // 8 * (rows // 128)
-    return depth < 8 and depth % 2 == 0 and mesh_y % 4 == 0 and tiles % (2 * mesh_z) == 0
+    tiles = 2 * depth // 8 * (rows // 128)
+    return depth == 4 and mesh_y % 4 == 0 and tiles % (2 * mesh_z) == 0
 
 
 def wave_rows(length):
@@ -566,11 +566,29 @@
         self.steps = self.half // 128
         self.tiers = self.bins // 8
         self.lanes = self.rows // 128
-        self.tiles = 4 * self.depth // 8 * self.lanes
+        self.tiles = 2 * self.depth // 8 * self.lanes
         self.share = self.tiles // (2 * self.nz)
 
     def place_of(self, index):
         return (lax.rem(index, self.ny), lax.div(index, self.ny))
+
+    def find_place(self):
+        self.y, self.z = (lax.axis_index("gy"), lax.axis_index("gz"))
+        self.me = self.z * self.ny + self.y
+
+        def turned(place, count):
+            moved = [place + k for k in range(count)]
+            return [jnp.where(item >= count, item - count, item) for item in moved]
+
+        ys, zs = (turned(self.y, self.ny), turned(self.z, self.nz))
+        far = sorted(range(self.ny), key=lambda k: -min(k, self.ny - k))
+        self.cuts = (self.nd // 16, self.nd // 2, self.nd * 7 // 8)
+        self.peers = [(ys[a], zs[b]) for a in far for b in reversed(range(self.nz)) if a or b]
+
+    def remote_to(self, source, target, send, receive, place):
+        return pltpu.make_async_remote_copy(
+            src_ref=source, dst_ref=target, send_sem=send, recv_sem=receive, device_id=place, device_id_type=MESH
+        )
 
     def scratch(self):
         Z, bins, half, nd = (self.depth, self.bins, self.half, self.nd)
@@ -619,24 +637,29 @@
             cols_m1=pltpu.VMEM((2, 8, self.rows), F),
             cols_mw=pltpu.VMEM((2, 8, self.rows), F),
             edge_cols=pltpu.VMEM((2, 8, self.rows), F),
-            part=pltpu.VMEM((3, 3, self.tiles, 8, 128), F),
-            slots=pltpu.VMEM((3, 3, others, self.share, 8, 128), F),
-            sums=pltpu.VMEM((3, 3, self.share, 8, 128), F),
-            full=pltpu.VMEM((3, 3, self.tiles, 8, 128), F),
+            part=pltpu.VMEM((3, 5, self.tiles, 8, 128), F),
+            slots=pltpu.VMEM((3, 5, others, self.share, 8, 128), F),
+            sums=pltpu.VMEM((3, 5, self.share, 8, 128), F),
+            full=pltpu.VMEM((3, 5, self.tiles, 8, 128), F),
+            line_part=pltpu.VMEM((3, 1, 128), F),
+            line_slots=pltpu.VMEM((3, others, 1, 128), F),
+            line_sums=pltpu.VMEM((3, 1, 128), F),
+            line_full=pltpu.VMEM((3, 1, 128), F),
+            around=pltpu.VMEM(field, F),
             acc=pltpu.VMEM((8, 8, 128), F),
             taps=pltpu.VMEM((27, 8, 128), F),
             tap_part=pltpu.VMEM((1, 128), F),
             tap_slots=pltpu.VMEM((nd, 1, 128), F),
             sent_o=pltpu.VMEM(packed, F),
             got_o=pltpu.VMEM((nd, 2, bins, self.row_count), F),
-            send_big=D((3,)),
-            recv_big=D((3,)),
+            send_big=D((4,)),
+            recv_big=D((4,)),
             send_p=D,
             recv_p=D,
-            send_part=D((2, 3)),
-            recv_part=D((2, 3)),
-            send_full=D((2, 3)),
-            recv_full=D((2, 3)),
+            send_part=D((2, 5)),
+            recv_part=D((2, 5)),
+            send_full=D((2, 5)),
+            recv_full=D((2, 5)),
             send_tap=D,
             recv_tap=D,
         )
@@ -655,18 +678,11 @@
     def row_lanes(self, y):
         return pl.ds(pl.multiple_of(y * self.row_count, 128), self.row_count)
 
-    def spread_start(self, r, sent, got, lot, quarter=None):
-        first, end = (1, self.nd)
-        if quarter is not None:
-            first, end = (max(1, quarter * self.nd // 4), (quarter + 1) * self.nd // 4)
+    def spread_start(self, r, sent, got, lot, first=0, end=None):
         here = got.at[self.z, :, :, self.row_lanes(self.y)]
-
-        @pl.loop(first, end)
-        def _(k):
-            peer = lax.rem(self.me + k, self.nd)
-            self.remote(sent.at[peer], here, r.send_big.at[lot], r.recv_big.at[lot], peer).start()
-
-        if not quarter:
+        for y, z in self.peers[first:end]:
+            self.remote_to(sent.at[z * self.ny + y], here, r.send_big.at[lot], r.recv_big.at[lot], (y, z)).start()
+        if first == 0:
             here[...] = sent[self.me]
 
     def spread_wait(self, r, sent, lot):
@@ -689,16 +705,11 @@
         self.arrived(others, r.recv_p)
         self.arrived(others, r.send_p)
 
-    def return_start(self, r):
-        @pl.loop(1, self.nd)
-        def _(k):
-            peer = lax.rem(self.me + k, self.nd)
-            y, z = self.place_of(peer)
-            self.remote(
-                r.sent_o.at[z, :, :, self.row_lanes(y)], r.got_o.at[self.me], r.send_big.at[2], r.recv_big.at[2], peer
+    def return_start(self, r, first, end):
+        for y, z in self.peers[first:end]:
+            self.remote_to(
+                r.sent_o.at[z, :, :, self.row_lanes(y)], r.got_o.at[self.me], r.send_big.at[2], r.recv_big.at[2], (y, z)
             ).start()
-
-        r.got_o[self.me] = r.sent_o[self.z, :, :, self.row_lanes(self.y)]
 
     def owner(self, kind, number):
         if kind == 2:
@@ -720,12 +731,15 @@
     def width(self, kind):
         return 1 if kind == 2 else self.share
 
-    def lot(self, ref, turn, kind, number, count=1):
-        count = count * self.width(kind)
-        return ref.at[turn, kind, pl.ds(number * self.width(kind), count)]
+    def lot(self, r, name, turn, kind, number, count=1):
+        if kind == 2:
+            return getattr(r, "line_" + name).at[turn]
+        return getattr(r, name).at[turn, kind, pl.ds(number * self.share, count * self.share)]
 
     def slot(self, r, turn, kind, first, count=1):
-        return r.slots.at[turn, kind, pl.ds(first, count), pl.ds(0, self.width(kind))]
+        if kind == 2:
+            return r.line_slots.at[turn, pl.ds(first, count)]
+        return r.slots.at[turn, kind, pl.ds(first, count)]
 
     def reduce_start(self, r, turn, kinds):
         for kind in kinds:
@@ -739,7 +753,7 @@
                 def _():
                     place = lax.rem(self.me - owner + self.nd, self.nd) - 1
                     self.remote(
-                        self.lot(r.part, turn, kind, number), self.slot(r, turn, kind, place).at[0], send, receive, owner
+                        self.lot(r, "part", turn, kind, number), self.slot(r, turn, kind, place).at[0], send, receive, owner
                     ).start()
 
     def reduce_middle(self, r, turn, kinds):
@@ -751,20 +765,16 @@
             def _():
                 number = self.mine(kind)
                 self.arrived(self.slot(r, turn, kind, 0, others), r.recv_part.at[turn % 2, kind])
-                lots = [self.lot(r.part, turn, kind, number)[...]]
+                lots = [self.lot(r, "part", turn, kind, number)[...]]
                 lots += [self.slot(r, turn, kind, k)[0] for k in range(others)]
                 while len(lots) > 1:
                     lots = [lots[k] + lots[k + 1] for k in range(0, len(lots) - 1, 2)] + lots[len(lots) // 2 * 2 :]
-                sums = r.sums.at[turn, kind, pl.ds(0, self.width(kind))]
+                sums = self.lot(r, "sums", turn, kind, 0)
                 sums[...] = lots[0]
-
-                @pl.loop(1, self.nd)
-                def _(k):
-                    self.remote(
-                        sums, self.lot(r.full, turn, kind, number), send, receive, lax.rem(self.me + k, self.nd)
-                    ).start()
-
-                self.lot(r.full, turn, kind, number)[...] = lots[0]
+                full = self.lot(r, "full", turn, kind, number)
+                for place in self.peers:
+                    self.remote_to(sums, full, send, receive, place).start()
+                full[...] = lots[0]
 
     def reduce_end(self, r, turn, kinds):
         for kind in kinds:
@@ -772,8 +782,8 @@
 
             def finish(count):
                 if count:
-                    self.arrived(self.lot(r.full, turn, kind, 0, count), r.recv_full.at[turn % 2, kind])
-                    self.arrived(self.lot(r.part, turn, kind, 0, count), r.send_part.at[turn % 2, kind])
+                    self.arrived(self.lot(r, "full", turn, kind, 0, count), r.recv_full.at[turn % 2, kind])
+                    self.arrived(self.lot(r, "part", turn, kind, 0, count), r.send_part.at[turn % 2, kind])
 
             @pl.when(self.owned(kind))
             def _():
@@ -943,13 +953,14 @@
                 key = (x, z, side)
                 columns[key] = term if key not in columns else columns[key] + term
 
-    def put_columns(self, part, tier, step, columns):
+    def put_columns(self, r, turn, kinds, tier, step, columns):
         if tier < self.tiers - 1:
             return
         for (x, z, side), value in columns.items():
-            index = x * self.depth + z
+            index = x // 2 * self.depth + z
+            kind = kinds[0] if x in (0, 3) else kinds[1]
             tile = index // 8 * self.lanes + side * self.steps + step
-            part[tile, pl.ds(index % 8, 1)] = jnp.sum(value, 0, keepdims=True)
+            r.part[turn, kind, tile, pl.ds(index % 8, 1)] = jnp.sum(value, 0, keepdims=True)
 
     def clear(self, *refs):
         for ref in refs:
@@ -959,14 +970,13 @@
         for k in range(2):
             rows[k] = jnp.broadcast_to(jnp.sum(rows[k], -1, keepdims=True), rows.shape[1:])
 
-    def unpack(self, full, cols):
+    def unpack(self, r, turn, kind, cols, inner):
         Z = self.depth
-        cols[...] = jnp.zeros(cols.shape, jnp.float32)
-        for x in range(4):
-            first = x * Z
+        for x in (1, 2) if inner else (0, 3):
+            first = x // 2 * Z
             for lane in range(self.lanes):
-                cols[x, pl.ds(0, Z), pl.ds(lane * 128, 128)] = full[
-                    first // 8 * self.lanes + lane, pl.ds(first % 8, Z)
+                cols[x, pl.ds(0, Z), pl.ds(lane * 128, 128)] = r.full[
+                    turn, kind, first // 8 * self.lanes + lane, pl.ds(first % 8, Z)
                 ]
 
     def shifted(self, value, by):
@@ -983,56 +993,43 @@
             out.append(jnp.broadcast_to(jnp.sum(col * weight, -1, keepdims=True), (8, 128)))
         return out
 
-    def edges(self, r, w, rows, col_first, col_last, inner=None, mapped=None):
+    def column_tools(self, r, w, step):
+        c = [self.along(r, COS, step, part) for part in range(2)]
+        s = self.along(r, SIN, step, 0)
+        first = [self.along(r, FIRST, step, part) for part in range(2)]
+        last = [self.along(r, LAST, step, part) for part in range(2)]
+
+        def get(col):
+            return [col[:, self.lane_slice(step, part)] for part in range(2)]
+
+        def line(a, c_index, col):
+            w0, w1, w2 = (w(a, b, c_index) for b in range(3))
+            turn = (w2 - w0) * s
+            return [
+                (w1 + (w0 + w2) * c[0]) * col[0] + turn * col[1],
+                (w1 + (w0 + w2) * c[1]) * col[1] - turn * col[0],
+            ]
+
+        def stacked(pieces):
+            out = None
+            for a in range(3):
+                for c_index, col in pieces:
+                    term = [self.shifted(part, a - 1) for part in line(a, c_index, col)]
+                    out = term if out is None else [p + t for p, t in zip(out, term)]
+            return out
+
+        return (first, last, get, stacked)
+
+    def edges(self, r, w, col_first, col_last):
         Z = self.depth
         k_first, k_last = (self.corners(r, col_first[...]), self.corners(r, col_last[...]))
         total = lambda terms: sum(terms[1:], terms[0])
         q = {}
         for name, b, c, value in ((0, 0, 0, k_last[1]), (1, 0, 2, k_first[1]), (2, 2, 0, k_last[0]), (3, 2, 2, k_first[0])):
             q[name] = total([w(a, b, c) * self.shifted(value, a - 1) for a in range(3)])
-        if inner is not None:
-            near, far = inner
-            k_near, k_far = (self.corners(r, near[...]), self.corners(r, far[...]))
-            fix = []
-            for (c0, v0), (c1, v1) in (((1, k_first), (2, k_near)), ((0, k_far), (1, k_last))):
-                fix.append(
-                    [
-                        total(
-                            [
-                                w(a, b, c0) * self.shifted(v0[y], a - 1) + w(a, b, c1) * self.shifted(v1[y], a - 1)
-                                for a in range(3)
-                            ]
-                        )
-                        for b, y in ((0, 1), (2, 0))
-                    ]
-                )
-
         @pl.loop(0, self.steps)
         def _(step):
-            c = [self.along(r, COS, step, part) for part in range(2)]
-            s = self.along(r, SIN, step, 0)
-            first = [self.along(r, FIRST, step, part) for part in range(2)]
-            last = [self.along(r, LAST, step, part) for part in range(2)]
-
-            def get(col):
-                return [col[:, self.lane_slice(step, part)] for part in range(2)]
-
-            def line(a, c_index, col):
-                w0, w1, w2 = (w(a, b, c_index) for b in range(3))
-                turn = (w2 - w0) * s
-                return [
-                    (w1 + (w0 + w2) * c[0]) * col[0] + turn * col[1],
-                    (w1 + (w0 + w2) * c[1]) * col[1] - turn * col[0],
-                ]
-
-            def stacked(pieces):
-                out = None
-                for a in range(3):
-                    for c_index, col in pieces:
-                        term = [self.shifted(part, a - 1) for part in line(a, c_index, col)]
-                        out = term if out is None else [p + t for p, t in zip(out, term)]
-                return out
-
+            first, last, get, stacked = self.column_tools(r, w, step)
             f, l = (get(col_first), get(col_last))
             for k, (pieces, upper, lower) in enumerate((([(0, l)], q[0], q[2]), ([(2, f)], q[1], q[3]))):
                 value = stacked(pieces)
@@ -1040,15 +1037,9 @@
                     r.edge_cols[k, :, self.lane_slice(step, part)] = (
                         value[part] - upper * first[part] - lower * last[part]
                     )
-            if inner is not None:
-                n, g = (get(near), get(far))
-                for k, pieces in enumerate(([(1, f), (2, n)], [(0, g), (1, l)])):
-                    value = stacked(pieces)
-                    for part in range(2):
-                        mapped[k, :, self.lane_slice(step, part)] = (
-                            value[part] - fix[k][0] * first[part] - fix[k][1] * last[part]
-                        )
-
+
+    def edge_lines(self, r, w, rows):
+        Z = self.depth
         for tier in range(self.tiers):
             here = pl.ds(8 * tier, 8)
             c = [self.beside(r, COS, part, tier) for part in range(2)]
@@ -1070,6 +1061,36 @@
                     for part in range(2):
                         r.edge_rows[k, z, part, here] = out[part]
 
+    def map_columns(self, r, w, cols, mapped, extra=None):
+        total = lambda terms: sum(terms[1:], terms[0])
+        at = [self.corners(r, cols[x]) for x in range(4)]
+        fix = []
+        for (c0, v0), (c1, v1) in (((1, at[0]), (2, at[1])), ((0, at[2]), (1, at[3]))):
+            fix.append(
+                [
+                    total(
+                        [
+                            w(a, b, c0) * self.shifted(v0[y], a - 1) + w(a, b, c1) * self.shifted(v1[y], a - 1)
+                            for a in range(3)
+                        ]
+                    )
+                    for b, y in ((0, 1), (2, 0))
+                ]
+            )
+
+        @pl.loop(0, self.steps)
+        def _(step):
+            first, last, get, stacked = self.column_tools(r, w, step)
+            f, n, g, l = (get(cols.at[x]) for x in range(4))
+            for k, pieces in enumerate(([(1, f), (2, n)], [(0, g), (1, l)])):
+                value = stacked(pieces)
+                for part in range(2):
+                    here = (k, slice(None), self.lane_slice(step, part))
+                    value_here = value[part] - fix[k][0] * first[part] - fix[k][1] * last[part]
+                    if extra is not None:
+                        value_here = value_here + extra(here)
+                    mapped[here] = value_here
+
     def edge_field(self, r, masks, tier, step, z):
         here = pl.ds(8 * tier, 8)
         out = []
@@ -1082,19 +1103,28 @@
                 out.append(e0 * y0 + e1 * y1 + x0 * c0 + x1 * c1)
         return self.combine(masks, *out)
 
-    def stencil_field(self, r, masks, tier, step, field, flip):
+    def circular_field(self, r, tier, step, field, flip, out=None):
         Z = self.depth
         value = [self.load(field, z, tier, step) for z in range(Z)]
-        out = [[-e for e in self.edge_field(r, masks, tier, step, z)] for z in range(Z)]
+        out = [None] * Z if out is None else out
         for a in range(3):
-            where = (pl.ds(8 * tier, 8), self.lane_slice(step))
-            factor = [[r.stencil[(a, side, k) + where] for k in range(3)] for side in range(2)]
+            factor = self.factor(r.stencil.at[a], tier, step)
             for z in range(Z):
                 other = z + (1 - a if flip else a - 1)
                 if 0 <= other < Z:
                     term = self.times(factor, value[other], flip)
-                    out[z] = [o + t for o, t in zip(out[z], term)]
+                    out[z] = term if out[z] is None else [o + t for o, t in zip(out[z], term)]
         return out
+
+    def turn_round(self, r, field, out, norm=None):
+        def body(tier, step, masks, columns):
+            for z, value in enumerate(self.circular_field(r, tier, step, field, False)):
+                self.keep(out, z, tier, step, value)
+                if norm is not None:
+                    own = self.load(field, z, tier, step)
+                    norm[...] += self.dot(masks, own, own)
+
+        self.sweep(body)
 
     def build_stencil(self, r, w):
         def body(tier, step, masks, columns):
@@ -1153,53 +1183,55 @@
         return jnp.where(corner, 0.5 * total, total)
 
 
-    def stencil_twice(self, r, w, field, rows, cols, mapped, rows_m, cols_m, finish, after=None):
+    def stencil_twice(self, r, w, cols, mapped, rows_m, cols_m, make, finish, inner, extra=None):
         def flipped(a, b, c):
             return w(2 - a, 2 - b, 2 - c)
 
-        self.edges(r, w, rows, cols.at[0], cols.at[3], (cols.at[1], cols.at[2]), cols_m)
+        self.edges(r, w, cols.at[0], cols.at[3])
         self.clear(rows_m)
 
         def forward(tier, step, masks, columns):
-            out = self.stencil_field(r, masks, tier, step, field, False)
             for z in range(self.depth):
-                self.keep(mapped, z, tier, step, out[z])
-                self.frames(r, masks, tier, step, z, out[z], rows_m)
+                value = [m - e for m, e in zip(make(tier, step, z), self.edge_field(r, masks, tier, step, z))]
+                self.keep(mapped, z, tier, step, value)
+                self.frames(r, masks, tier, step, z, value, rows_m)
 
         self.sweep(forward)
         self.settle(rows_m)
-        self.edges(r, flipped, rows_m, cols_m.at[0], cols_m.at[1])
+        inner()
+        self.map_columns(r, w, cols, cols_m, extra)
+        self.edge_lines(r, flipped, rows_m)
+        self.edges(r, flipped, cols_m.at[0], cols_m.at[1])
 
         def back(tier, step, masks, columns):
-            finish(tier, step, masks, columns, self.stencil_field(r, masks, tier, step, mapped, True))
+            out = [[-e for e in self.edge_field(r, masks, tier, step, z)] for z in range(self.depth)]
+            finish(tier, step, masks, columns, self.circular_field(r, tier, step, mapped, True, out))
 
         self.sweep(back)
 
     def scalars_out(self, r, turn, count):
+        lane = lax.broadcasted_iota(jnp.int32, (1, 128), 1)
+        line = jnp.zeros((1, 128), jnp.float32)
         for k in range(count):
-            r.part[turn, 2, 0, pl.ds(k, 1)] = jnp.sum(r.acc[k], 0, keepdims=True)
-        for k in range(count, 8):
-            r.part[turn, 2, 0, pl.ds(k, 1)] = jnp.zeros((1, 128), jnp.float32)
+            whole = jnp.sum(jnp.sum(r.acc[k], 0, keepdims=True), -1, keepdims=True)
+            line = jnp.where(lane == k, whole, line)
+        r.line_part[turn] = line
 
     def scalars_in(self, r, turn, count):
-        value = jnp.sum(r.full[turn, 2, 0], -1, keepdims=True)
-        return [jnp.broadcast_to(value[k : k + 1], (8, 128)) for k in range(count)]
+        line = r.line_full[turn]
+        return [jnp.broadcast_to(line[:, k : k + 1], (8, 128)) for k in range(count)]
 
     def run(self, r):
         Z = self.depth
-        self.y, self.z = (lax.axis_index("gy"), lax.axis_index("gz"))
-        self.me = self.z * self.ny + self.y
+        self.find_place()
 
         def w(a, b, c):
             return r.weights[a, b, c]
 
         barrier = pltpu.get_barrier_semaphore()
 
-        @pl.loop(1, self.nd)
-        def _(k):
-            pl.semaphore_signal(
-                barrier, inc=1, device_id=self.place_of(lax.rem(self.me + k, self.nd)), device_id_type=MESH
-            )
+        for place in self.peers:
+            pl.semaphore_signal(barrier, inc=1, device_id=place, device_id_type=MESH)
 
         def load(name):
             far = getattr(r, "far_" + name)
@@ -1231,12 +1263,13 @@
         load("upstream").wait()
         self.row_spectra(r, r.upstream[0], r.sent_u)
         self.clear(r.rows_v0, r.rows_v1, r.rows_v2, r.rows_up, r.acc, r.taps)
+        self.clear(r.cols_v0, r.cols_v1, r.cols_v2, r.cols_up)
 
         self.point_wait(r)
         self.column_spectra(r, r.got_p, r.wave_p)
         self.build_blur(r)
         self.spread_wait(r, r.sent_m, 0)
-        self.spread_start(r, r.sent_u, r.got_u, 1, 0)
+        self.spread_start(r, r.sent_u, r.got_u, 1, 0, self.cuts[0])
         self.column_spectra(r, r.got_m, r.wave)
 
         def start(tier, step, masks, columns):
@@ -1246,16 +1279,22 @@
                 value = self.times(factor, value, True)
                 self.keep(r.v0, z, tier, step, value)
                 self.frames(r, masks, tier, step, z, value, r.rows_v0, columns)
-            self.put_columns(r.part.at[0, 0], tier, step, columns)
+            self.put_columns(r, 0, (0, 1), tier, step, columns)
 
         self.sweep(start)
-        self.reduce_start(r, 0, [0])
-        self.spread_start(r, r.sent_u, r.got_u, 1, 1)
+        self.reduce_start(r, 0, [0, 1])
         self.settle(r.rows_v0)
-        self.reduce_middle(r, 0, [0])
+        self.edge_lines(r, w, r.rows_v0)
+        self.reduce_middle(r, 0, [0, 1])
+        self.spread_start(r, r.sent_u, r.got_u, 1, self.cuts[0], self.cuts[1])
+        self.turn_round(r, r.v0, r.m0, r.acc.at[0])
         self.reduce_end(r, 0, [0])
-        self.spread_start(r, r.sent_u, r.got_u, 1, 2)
-        self.unpack(r.full.at[0, 0], r.cols_v0)
+        self.unpack(r, 0, 0, r.cols_v0, False)
+        self.spread_start(r, r.sent_u, r.got_u, 1, self.cuts[1], self.cuts[2])
+
+        def inner_0():
+            self.reduce_end(r, 0, [1])
+            self.unpack(r, 0, 1, r.cols_v0, True)
 
         def first(tier, step, masks, columns, back):
             for z in range(Z):
@@ -1263,17 +1302,24 @@
                 value = [g + b for g, b in zip(self.gained(r, tier, step, before), back[z])]
                 self.keep(r.v1, z, tier, step, value)
                 self.frames(r, masks, tier, step, z, value, r.rows_v1, columns)
-                r.acc[0] += self.dot(masks, before, before)
                 r.acc[1] += self.dot(masks, before, value)
                 r.acc[2] += self.dot(masks, value, value)
-            self.put_columns(r.part.at[1, 0], tier, step, columns)
-
-        self.stencil_twice(r, w, r.v0, r.rows_v0, r.cols_v0, r.m0, r.rows_m0, r.cols_m0, first)
+            self.put_columns(r, 1, (0, 1), tier, step, columns)
+
+        def plain(field):
+            return lambda tier, step, z: self.load(field, z, tier, step)
+
+        self.stencil_twice(
+            r, w, r.cols_v0, r.m0, r.rows_m0, r.cols_m0, plain(r.m0), first, inner_0
+        )
+        self.reduce_start(r, 1, [0])
         self.scalars_out(r, 1, 3)
-        self.reduce_start(r, 1, [0, 2])
-        self.spread_start(r, r.sent_u, r.got_u, 1, 3)
+        self.reduce_start(r, 1, [1, 2])
         self.settle(r.rows_v1)
-        self.reduce_middle(r, 1, [0, 2])
+        self.edge_lines(r, w, r.rows_v1)
+        self.reduce_middle(r, 1, [0, 1, 2])
+        self.spread_start(r, r.sent_u, r.got_u, 1, self.cuts[2])
+        self.turn_round(r, r.v1, r.m1)
         self.spread_wait(r, r.sent_u, 1)
         self.column_spectra(r, r.got_u, r.wave)
 
@@ -1282,42 +1328,57 @@
                 value = self.combine(masks, *self.load_wave(r.wave, z, tier, step))
                 self.keep(r.up, z, tier, step, value)
                 self.frames(r, masks, tier, step, z, value, r.rows_up, columns)
-            self.put_columns(r.part.at[2, 1], tier, step, columns)
-
+                r.acc[5] += self.dot(masks, value, self.load(r.v0, z, tier, step))
+                r.acc[6] += self.dot(masks, value, self.load(r.v1, z, tier, step))
+            self.put_columns(r, 2, (3, 4), tier, step, columns)
+
+        self.clear(r.acc)
         self.sweep(upper)
         self.settle(r.rows_up)
-        self.clear(r.acc)
-        self.reduce_end(r, 1, [0, 2])
-        self.reduce_start(r, 2, [1])
-        self.unpack(r.full.at[1, 0], r.cols_v1)
-        norm_0, curve_0, image_0 = self.scalars_in(r, 1, 3)
-        step_0 = norm_0 / curve_0
+        self.reduce_end(r, 1, [0])
+        self.unpack(r, 1, 0, r.cols_v1, False)
+        scalars = []
+
+        def inner_1():
+            self.reduce_end(r, 1, [1, 2])
+            self.unpack(r, 1, 1, r.cols_v1, True)
+            self.reduce_start(r, 2, [3, 4])
+            scalars.extend(self.scalars_in(r, 1, 3))
+            scalars.append(scalars[0] / scalars[1])
 
         def second(tier, step, masks, columns, back):
             for z in range(Z):
                 before, value = (self.load(f, z, tier, step) for f in (r.v0, r.v1))
-                up = self.load(r.up, z, tier, step)
                 after = [g + b for g, b in zip(self.gained(r, tier, step, value), back[z])]
                 self.keep(r.v2, z, tier, step, after)
                 self.frames(r, masks, tier, step, z, after, r.rows_v2, columns)
+                step_0 = scalars[3]
                 residual = [p - step_0 * q for p, q in zip(before, value)]
                 image = [p - step_0 * q for p, q in zip(value, after)]
                 for k, (p, q) in enumerate(
-                    ((residual, residual), (residual, value), (residual, image), (image, value), (up, residual), (up, before), (up, value))
+                    ((residual, residual), (residual, value), (residual, image), (image, value))
                 ):
                     r.acc[k] += self.dot(masks, p, q)
-            self.put_columns(r.part.at[2, 0], tier, step, columns)
-
-        self.stencil_twice(r, w, r.v1, r.rows_v1, r.cols_v1, r.m1, r.rows_m1, r.cols_m1, second)
+            self.put_columns(r, 2, (0, 1), tier, step, columns)
+
+        self.stencil_twice(
+            r, w, r.cols_v1, r.m1, r.rows_m1, r.cols_m1, plain(r.m1), second, inner_1
+        )
+        norm_0, curve_0, image_0, step_0 = scalars
         self.scalars_out(r, 2, 7)
-        self.reduce_start(r, 2, [0, 2])
+        self.reduce_start(r, 2, [2, 0, 1])
         self.settle(r.rows_v2)
-        self.reduce_middle(r, 2, [1, 0, 2])
-        self.reduce_end(r, 2, [1, 0, 2])
-        self.unpack(r.full.at[2, 0], r.cols_v2)
-        self.unpack(r.full.at[2, 1], r.cols_up)
-
-        norm_1, cross, inner, image_cross, up_residual, up_0, up_1 = self.scalars_in(r, 2, 7)
+        self.reduce_middle(r, 2, [3, 4, 2, 0, 1])
+        self.turn_round(r, r.up, r.around)
+        self.turn_round(r, r.v2, r.mw)
+        self.reduce_end(r, 2, [3, 4])
+        self.unpack(r, 2, 3, r.cols_up, False)
+        self.unpack(r, 2, 4, r.cols_up, True)
+        self.reduce_end(r, 2, [2, 0])
+        self.unpack(r, 2, 0, r.cols_v2, False)
+
+        norm_1, cross, inner, image_cross, unused, up_0, up_1 = self.scalars_in(r, 2, 7)
+        up_residual = up_0 - step_0 * up_1
         ratio = norm_1 / norm_0
         curve_1 = inner + 2.0 * ratio * cross + ratio * ratio * curve_0
         step_1 = norm_1 / curve_1
@@ -1338,30 +1399,38 @@
         mix = (g1, 2.0 * g2, 2.0 * g3, q1)
 
         def mixed(*values):
-            return mix[0] * values[0] + mix[1] * values[1] + mix[2] * values[2] + mix[3] * values[3]
-
-        for x in range(4):
-
-            @pl.loop(0, self.lanes)
-            def _(lane):
-                here = (x, slice(None), pl.ds(pl.multiple_of(lane * 128, 128), 128))
-                r.cols_w3[here] = mixed(*(f[here] for f in (r.cols_v0, r.cols_v1, r.cols_v2, r.cols_up)))
-
+            return sum(m * v for m, v in zip(mix[4 - len(values) :], values))
+
+        def mix_columns(places):
+            for x in places:
+                for lane in range(self.lanes):
+                    here = (x, slice(None), pl.ds(lane * 128, 128))
+                    r.cols_w3[here] = mixed(r.cols_v2[here], r.cols_up[here])
+
+        mix_columns((0, 3))
         for k in range(2):
             for part in range(2):
                 for tier in range(self.tiers):
-
-                    @pl.loop(0, Z)
-                    def _(z):
+                    for z in range(Z):
                         here = (k, z, part, pl.ds(8 * tier, 8))
-                        r.rows_w3[here] = mixed(*(f[here] for f in (r.rows_v0, r.rows_v1, r.rows_v2, r.rows_up)))
-
-        def blend(tier, step, masks, columns):
-            for z in range(Z):
-                values = [self.load(f, z, tier, step) for f in (r.v0, r.v1, r.v2, r.up)]
-                self.keep(r.w3, z, tier, step, [mixed(*parts) for parts in zip(*values)])
-
-        self.sweep(blend)
+                        r.rows_w3[here] = mixed(r.rows_v2[here], r.rows_up[here])
+
+        self.edge_lines(r, w, r.rows_w3)
+
+        def inner_2():
+            self.reduce_end(r, 2, [1])
+            self.unpack(r, 2, 1, r.cols_v2, True)
+            mix_columns((1, 2))
+
+        def make(tier, step, z):
+            values = [self.load(f, z, tier, step) for f in (r.v0, r.v1, r.v2, r.up)]
+            self.keep(r.w3, z, tier, step, [mixed(*parts) for parts in zip(*values)])
+            values = [self.load(f, z, tier, step) for f in (r.m0, r.m1, r.mw, r.around)]
+            return [mixed(*parts) for parts in zip(*values)]
+
+        def extra(here):
+            return mix[0] * r.cols_m0[here] + mix[1] * r.cols_m1[here]
+
         scale = 1.0 / (self.rows * self.columns)
 
         def last(tier, step, masks, columns, back):
@@ -1381,17 +1450,23 @@
                             value[2 * part + side] * heavy * self.along(r, WEIGHT, step, side)
                         )
 
-        self.stencil_twice(r, w, r.w3, r.rows_w3, r.cols_w3, r.mw, r.rows_mw, r.cols_mw, last)
+        self.stencil_twice(
+            r, w, r.cols_w3, r.mw, r.rows_mw, r.cols_mw, make, last, inner_2, extra
+        )
         self.column_values(r, r.wave, r.sent_o)
-
-        self.return_start(r)
+        middle = len(self.peers) // 2
+        self.return_start(r, 0, middle)
+        for k in range(2):
+            for x in (0, 3):
+                if k == 0:
+                    r.cols_w3[x] = r.cols_w3[x] + self.blend(mix, r.cols_v0[x], r.cols_v1[x])
+            r.rows_w3[k] = r.rows_w3[k] + self.blend(mix, r.rows_v0[k], r.rows_v1[k])
         self.tap_sums(r, 2.0 * g3)
 
-        @pl.loop(1, self.nd)
-        def _(k):
-            peer = lax.rem(self.me + k, self.nd)
-            self.remote(r.tap_part, r.tap_slots.at[self.me], r.send_tap, r.recv_tap, peer).start()
-
+        for place in self.peers:
+            self.remote_to(r.tap_part, r.tap_slots.at[self.me], r.send_tap, r.recv_tap, place).start()
+        self.return_start(r, middle, None)
+        r.got_o[self.me] = r.sent_o[self.z, :, :, self.row_lanes(self.y)]
         r.tap_slots[self.me] = r.tap_part[...]
         others = pl.ds(0, self.nd - 1)
         self.arrived(r.got_o.at[others], r.recv_big.at[2])
@@ -1408,6 +1483,9 @@
                 first = 9 * a + 3 * b
                 turned = pltpu.roll(line, 128 - first, 1) if first else line
                 r.tap_out[a, pl.ds(b, 1)] = turned[:1, :3]
+
+    def blend(self, mix, one, two):
+        return mix[0][:1, :1] * one + mix[1][:1, :1] * two
 
     def tap_sums(self, r, weight):
         Z = self.depth

time: 77.9 us -> 73.2 us (0.940)
  Pallas kernels: 75.6 us -> 70.8 us
    pallas_call x1, Pallas kernels: 75.6 us -> 70.8 us  [spectral(): pl.pallas_call(body, out_shape=(jax.ShapeDtypeStruct(measured.shape, jnp....]
where the time goes in v4:
time: 73.2 us; the launch traced here: 72.8 us
  Pallas kernels  70.8 us (97%)
  local copies, waits for them, and re-layouts  1.39 us (2%)
    pallas_call x1, Pallas kernels, spectral(): pl.pallas_call(body, out_shape=(jax.ShapeDtypeStruct(measured.shape, jnp....  70.8 us

profile of v4, /device:TPU:0, one launch (start us, length us, event | category | flops | bytes accessed | tf_op | source)
XLA Modules:
  0.0 72.8 jit_solution(11150337830567252091)
XLA Ops:
  0.6 70.8 %spectral.1 = (f32[1,128,1024]{2,1,0:T(8,128)S(1)}, f32[3,3,3]{2,1,0:T(4,128)S(1)}) custom-call(f32[3,3,3]{2,1,0:T(4,128)} %refs_0_.1, f32[1,128,1024]{2,1,0:T(8,128)} %refs_1_.1, f32[128,1024]{1,0:T(8,128)} %refs_2_.1, f32[1,128,1024]{2,1,0:T(8,128)} %refs_3_.1, f32[9,1,1024]{2,1,0:T(1,128)} %constant.10.clone.refs_4_, ...), custom_call_target="tpu_custom_call" | custom-call | tf_op jit(solution)/shard_map/spectral/pallas_call | solution.py:1647
  71.4 0.8 %copy.12 = f32[1,128,1024]{2,1,0:T(8,128)} copy(f32[1,128,1024]{2,1,0:T(8,128)S(1)} %get-tuple-element.4) | data formatting | bytes 1048576
  72.2 0.6 copy.13

commit v5 on v4

--- a/solution.py
+++ b/solution.py
@@ -647,6 +647,7 @@
             line_full=pltpu.VMEM((3, 1, 128), F),
             around=pltpu.VMEM(field, F),
             acc=pltpu.VMEM((8, 8, 128), F),
+            turned=pltpu.VMEM((2, 4, half, half // 2), jnp.bfloat16),
             taps=pltpu.VMEM((27, 8, 128), F),
             tap_part=pltpu.VMEM((1, 128), F),
             tap_slots=pltpu.VMEM((nd, 1, 128), F),
@@ -819,7 +820,12 @@
             table = tuple(half_table[2 * odd + part, pl.ds(start, block)] for half_table in r.tab_x)
             r.sent_p[:, part] = product(table, value, ((1,), (1,))).reshape(self.ny, self.bins, self.row_count)
 
-    def column_spectra(self, r, got, wave):
+    def turn_tables(self, r):
+        for k in range(2):
+            for part in range(4):
+                r.turned[k, part] = r.tab_y[k][part].astype(jnp.float32).T.astype(jnp.bfloat16)
+
+    def column_spectra(self, r, got, wave, turned=True):
         count = math.prod(got.shape[:-1])
         value = got[...].reshape(count, self.rows)
         low, high = (value[:, : self.half], value[:, self.half :])
@@ -827,9 +833,10 @@
         for odd, value in enumerate((low + high, low - high)):
             value = split(value)
             for part in range(2):
-                table = (r.tab_y[0][2 * odd + part], r.tab_y[1][2 * odd + part])
+                tables = (r.turned.at[0], r.turned.at[1]) if turned else r.tab_y
+                table = (tables[0][2 * odd + part], tables[1][2 * odd + part])
                 wave[..., pl.ds(part * self.half + odd * quarter, quarter)] = product(
-                    value, table, ((1,), (1,))
+                    value, table, ((1,), (0 if turned else 1,))
                 ).reshape(got.shape[:-1] + (quarter,))
 
     def column_values(self, r, wave, target):
@@ -1027,7 +1034,7 @@
         q = {}
         for name, b, c, value in ((0, 0, 0, k_last[1]), (1, 0, 2, k_first[1]), (2, 2, 0, k_last[0]), (3, 2, 2, k_first[0])):
             q[name] = total([w(a, b, c) * self.shifted(value, a - 1) for a in range(3)])
-        @pl.loop(0, self.steps)
+        @pl.loop(0, self.steps, unroll=True)
         def _(step):
             first, last, get, stacked = self.column_tools(r, w, step)
             f, l = (get(col_first), get(col_last))
@@ -1078,7 +1085,7 @@
                 ]
             )
 
-        @pl.loop(0, self.steps)
+        @pl.loop(0, self.steps, unroll=True)
         def _(step):
             first, last, get, stacked = self.column_tools(r, w, step)
             f, n, g, l = (get(cols.at[x]) for x in range(4))
@@ -1266,8 +1273,9 @@
         self.clear(r.cols_v0, r.cols_v1, r.cols_v2, r.cols_up)
 
         self.point_wait(r)
-        self.column_spectra(r, r.got_p, r.wave_p)
+        self.column_spectra(r, r.got_p, r.wave_p, False)
         self.build_blur(r)
+        self.turn_tables(r)
         self.spread_wait(r, r.sent_m, 0)
         self.spread_start(r, r.sent_u, r.got_u, 1, 0, self.cuts[0])
         self.column_spectra(r, r.got_m, r.wave)

time: 73.2 us -> 71.7 us (0.980)
  Pallas kernels: 70.8 us -> 69.3 us
    pallas_call x1, Pallas kernels: 70.8 us -> 69.3 us  [spectral(): pl.pallas_call(body, out_shape=(jax.ShapeDtypeStruct(measured.shape, jnp....]
where the time goes in v5:
time: 71.7 us; the launch traced here: 71.3 us
  Pallas kernels  69.3 us (97%)
  local copies, waits for them, and re-layouts  1.39 us (2%)
    pallas_call x1, Pallas kernels, spectral(): pl.pallas_call(body, out_shape=(jax.ShapeDtypeStruct(measured.shape, jnp....  69.3 us

profile of v5, /device:TPU:0, one launch (start us, length us, event | category | flops | bytes accessed | tf_op | source)
XLA Modules:
  0.0 71.3 jit_solution(9141385994416628902)
XLA Ops:
  0.6 69.3 %spectral.1 = (f32[1,128,1024]{2,1,0:T(8,128)S(1)}, f32[3,3,3]{2,1,0:T(4,128)S(1)}) custom-call(f32[3,3,3]{2,1,0:T(4,128)} %refs_0_.1, f32[1,128,1024]{2,1,0:T(8,128)} %refs_1_.1, f32[128,1024]{1,0:T(8,128)} %refs_2_.1, f32[1,128,1024]{2,1,0:T(8,128)} %refs_3_.1, f32[9,1,1024]{2,1,0:T(1,128)} %constant.10.clone.refs_4_, ...), custom_call_target="tpu_custom_call" | custom-call | tf_op jit(solution)/shard_map/spectral/pallas_call | solution.py:1655
  69.9 0.8 %copy.12 = f32[1,128,1024]{2,1,0:T(8,128)} copy(f32[1,128,1024]{2,1,0:T(8,128)S(1)} %get-tuple-element.4) | data formatting | bytes 1048576
  70.7 0.6 copy.13

commit v6 on v5

--- a/solution.py
+++ b/solution.py
@@ -582,7 +582,7 @@
 
         ys, zs = (turned(self.y, self.ny), turned(self.z, self.nz))
         far = sorted(range(self.ny), key=lambda k: -min(k, self.ny - k))
-        self.cuts = (self.nd // 16, self.nd // 2, self.nd * 7 // 8)
+        self.cuts = (self.nd // 16, self.nd * 9 // 16, self.nd * 7 // 8)
         self.peers = [(ys[a], zs[b]) for a in far for b in reversed(range(self.nz)) if a or b]
 
     def remote_to(self, source, target, send, receive, place):
@@ -866,7 +866,7 @@
             for part in range(2):
                 value = got[pl.ds(k * per, per), part].reshape(per * self.bins, self.row_count)
                 side = side + product(
-                    split(value.T), (r.tab_x[0][2 * k + part], r.tab_x[1][2 * k + part]), ((1,), (0,))
+                    split(value), (r.tab_x[0][2 * k + part], r.tab_x[1][2 * k + part]), ((0,), (0,))
                 )
             sides.append(side)
         half = self.columns // 2

time: 71.7 us -> 71.4 us (level)
  no operation moved by 1% of the time
where the time goes in v6:
time: 71.4 us; the launch traced here: 71 us
  Pallas kernels  69 us (97%)
  local copies, waits for them, and re-layouts  1.39 us (2%)
    pallas_call x1, Pallas kernels, spectral(): pl.pallas_call(body, out_shape=(jax.ShapeDtypeStruct(measured.shape, jnp....  69 us

profile of v6, /device:TPU:0, one launch (start us, length us, event | category | flops | bytes accessed | tf_op | source)
XLA Modules:
  0.0 71.0 jit_solution(5550618275621785680)
XLA Ops:
  0.6 69.0 %spectral.1 = (f32[1,128,1024]{2,1,0:T(8,128)S(1)}, f32[3,3,3]{2,1,0:T(4,128)S(1)}) custom-call(f32[3,3,3]{2,1,0:T(4,128)} %refs_0_.1, f32[1,128,1024]{2,1,0:T(8,128)} %refs_1_.1, f32[128,1024]{1,0:T(8,128)} %refs_2_.1, f32[1,128,1024]{2,1,0:T(8,128)} %refs_3_.1, f32[9,1,1024]{2,1,0:T(1,128)} %constant.10.clone.refs_4_, ...), custom_call_target="tpu_custom_call" | custom-call | tf_op jit(solution)/shard_map/spectral/pallas_call | solution.py:1655
  69.6 0.8 %copy.12 = f32[1,128,1024]{2,1,0:T(8,128)} copy(f32[1,128,1024]{2,1,0:T(8,128)S(1)} %get-tuple-element.4) | data formatting | bytes 1048576
  70.4 0.6 copy.13
